TPU v7x, 512 devices: a whole 4x8x8 slice. The times are simulated.
512 devices in a mesh: xz: 64 (over y, x, core), gy: 8 (over z).
Axes of the slice: x: 4, y: 8, z: 8, core: 2. Of those that a mesh axis runs over, the one named last changes fastest.
Arguments:
- initial_state: float32 [3, 2, 64, 512, 512], P(None, None, 'gy', 'xz'), may hold values from -6 to 6
- drag_rate: float32 [64, 512, 1024], P('gy', 'xz'), may hold values from 0.02 to 0.6
- wall_control: float32 [512, 1024], P('xz'), may hold values from -6 to 6
- lift_profile: float32 [64], replicated, may hold values from 0.05 to 0.3
- schur_inverse: float32 [64, 8, 512, 512], P('gy', None, 'xz'), may hold values from -1 to 3, as said below
Outputs:
- final_state: float32 [3, 2, 64, 512, 512], P(None, None, 'gy', 'xz')
- control_gradient: float32 [512, 1024], P('xz', 'gy')
Inputs may be any that keep to these rules, and one draw needn't show every extreme that they name: `schur_inverse`: each 8 x 8 block of one wavenumber holds the precomputed inverse of a Schur complement; dimension 1 indexes the block's columns.
All inputs are finite; a program needn't handle non-finite values.
Results may differ from a plain program's by a relative error of at most 0.00014.
Values sent between devices are 32-bit elements; how exact they have to be, the bound alone decides.
A program may use at most 128 MiB of HBM per device.

v0:
```python
import math

import jax
import jax.numpy as jnp
from jax import lax
from jax.sharding import PartitionSpec as P

STEPS = 2


DIFFUSION = 0.04
HIGHEST = lax.Precision.HIGHEST


def padded(cells, sides, width):
    for axis, dim in sides:
        count = lax.axis_size(axis)
        ends = count - 1
        head = lax.slice_in_dim(cells, 0, width, axis=dim)
        tail = lax.slice_in_dim(cells, cells.shape[dim] - width, cells.shape[dim], axis=dim)
        cells = jnp.concatenate(
            [
                lax.ppermute(tail, axis, [(i, (i + 1) % count) for i in range(ends)]),
                cells,
                lax.ppermute(head, axis, [((i + 1) % count, i) for i in range(ends)]),
            ],
            axis=dim,
        )
    return cells


def copy_for_each(shard, axis):
    copies = jnp.broadcast_to(shard, (lax.axis_size(axis), *shard.shape))
    return lax.all_to_all(copies, axis, split_axis=0, concat_axis=0, tiled=True)


def all_in_one(shard, axis):
    leaves = jax.tree.leaves(shard)
    sequence = sorted(range(len(leaves)), key=lambda k: -leaves[k].size)
    width = (1, *leaves[sequence[0]].shape)[-1]
    lines = [
        jnp.pad(leaves[k].reshape(-1), (0, -leaves[k].size % width)).reshape(-1, width)
        for k in sequence
    ]
    both, at, found = (copy_for_each(jnp.concatenate(lines), axis), 0, {})
    for k, line in zip(sequence, lines):
        share = both[:, at : at + len(line)].reshape(len(both), -1)
        found[k] = share[:, : leaves[k].size].reshape(-1, *leaves[k].shape)
        at += len(line)
    numbers = iter(range(len(leaves)))
    return jax.tree.map(lambda _: found[next(numbers)], shard)


def once_a_type(shard, axis):
    leaves, found = (jax.tree.leaves(shard), {})
    for initial, a in enumerate(leaves):
        if initial not in found:
            alike = [k for k, b in enumerate(leaves) if b.dtype == a.dtype]
            got = (
                all_in_one([leaves[k] for k in alike], axis)
                if len(alike) > 1
                else [copy_for_each(a, axis)]
            )
            for k, b in zip(alike, got):
                found[k] = b
    numbers = iter(range(len(leaves)))
    return jax.tree.map(lambda _: found[next(numbers)], shard)


def folded_in_pairs(pieces, combine):
    while len(jax.tree.leaves(pieces)[0]) > 1:
        pieces = jax.vmap(combine)(
            *(jax.tree.map(lambda part: part[side::2], pieces) for side in (0, 1))
        )
    return jax.tree.map(lambda part: part[0], pieces)


def prefix(shard, axis, combine, identity, reverse):
    count, index = (lax.axis_size(axis), lax.axis_index(axis))
    passed = jnp.arange(count) > index if reverse else jnp.arange(count) < index

    def kept(part, zero, own):
        part = jnp.where(
            passed.reshape(-1, *(1 for _ in own.shape)), part, jnp.asarray(zero, own.dtype)
        )
        return part[::-1] if reverse else part

    pieces = once_a_type(shard, axis)
    return folded_in_pairs(jax.tree.map(kept, pieces, identity, shard), combine)


def in_blocks(shard, dim, count):
    before, after = (shard.shape[:dim], shard.shape[dim + 1 :])
    return jnp.moveaxis(shard.reshape(*before, count, -1, *after), dim, 0)


def sent_and_summed(shard, axis, dim):
    count = lax.axis_size(axis)
    blocks = lax.all_to_all(in_blocks(shard, dim, count), axis, 0, 0, tiled=True)
    return jnp.sum(blocks, axis=0)


def take_rows(tensor, first_row, row_total):
    return lax.slice_in_dim(tensor, first_row, first_row + row_total, axis=tensor.ndim - 3)


def rotate(spectrum, factor):
    return jnp.stack([-factor * spectrum[1], factor * spectrum[0]])


def phase_pair(outer_size, inner_size, period, factor):
    outer_ids = jnp.arange(outer_size, dtype=jnp.int32)[:, None]
    inner_ids = jnp.arange(inner_size, dtype=jnp.int32)[None, :]
    angle = 2.0 * math.pi / period * (outer_ids * inner_ids % period).astype(jnp.float32)
    return (jnp.cos(angle) * factor, jnp.sin(angle) * factor)


def per_device(initial_state, drag_rate, wall_control, lift_profile, schur_inverse):
    row_count = initial_state.shape[2]
    mode_count = initial_state.shape[3]
    span_count = initial_state.shape[4]
    stream_len = drag_rate.shape[2]
    half_len = stream_len // 2
    slab_count = lax.axis_size("gy")
    slab_index = lax.axis_index("gy")
    pencil_index = lax.axis_index("xz")
    cos_x, sin_x = phase_pair(stream_len, half_len, stream_len, 1.0 / math.sqrt(stream_len))
    cos_z, sin_z = phase_pair(span_count, span_count, span_count, 1.0 / math.sqrt(span_count))
    all_modes = jnp.arange(half_len)
    weight_all = jnp.where(all_modes == 0, 1.0, 2.0).astype(jnp.float32)[:, None]
    mode_ids = pencil_index * mode_count + jnp.arange(mode_count)
    stream_factor = (2.0 * math.pi / stream_len * mode_ids.astype(jnp.float32))[:, None]
    mode_weight = jnp.where(mode_ids == 0, 1.0, 2.0).astype(jnp.float32)[:, None]
    span_ids = jnp.arange(span_count)
    signed = jnp.where(span_ids < span_count // 2, span_ids, span_ids - span_count)
    span_wave = jnp.where(
        span_ids == span_count // 2, 0.0, 2.0 * math.pi / span_count * signed.astype(jnp.float32)
    )
    wave_square = stream_factor**2 + span_wave[None, :] ** 2

    def to_spectral(physical):
        real_half = jnp.einsum("yzn,nk->yzk", physical, cos_x, precision=HIGHEST)
        imag_half = -jnp.einsum("yzn,nk->yzk", physical, sin_x, precision=HIGHEST)
        halfway = jnp.stack([real_half, imag_half])
        pieces = lax.all_to_all(halfway, "xz", split_axis=3, concat_axis=2, tiled=True)
        with_cos = jnp.einsum("cyzk,zq->cykq", pieces, cos_z, precision=HIGHEST)
        with_sin = jnp.einsum("cyzk,zq->cykq", pieces, sin_z, precision=HIGHEST)
        return jnp.stack([with_cos[0] + with_sin[1], with_cos[1] - with_sin[0]])

    def to_physical(spectral):
        with_cos = jnp.einsum("cykq,qz->cykz", spectral, cos_z, precision=HIGHEST)
        with_sin = jnp.einsum("cykq,qz->cykz", spectral, sin_z, precision=HIGHEST)
        halfway = jnp.stack([with_cos[0] - with_sin[1], with_sin[0] + with_cos[1]])
        weighted = (
            lax.all_to_all(halfway, "xz", split_axis=3, concat_axis=2, tiled=True) * weight_all
        )
        return jnp.einsum("ykz,nk->yzn", weighted[0], cos_x, precision=HIGHEST) - jnp.einsum(
            "ykz,nk->yzn", weighted[1], sin_x, precision=HIGHEST
        )

    def forward_drag(stream_part):
        return to_spectral(drag_rate * to_physical(stream_part))

    def adjoint_drag(stream_part):
        return mode_weight * to_spectral(drag_rate * to_physical(stream_part / mode_weight))

    padded_lift = jnp.pad(lift_profile, 1)
    lift_near = lax.dynamic_slice_in_dim(padded_lift, slab_index * row_count, row_count + 2)
    lift_own = lift_near[1 : row_count + 1]
    control_hat = to_spectral(wall_control[None])[:, 0]
    global_rows = slab_index * row_count - 1 + jnp.arange(row_count + 2)
    inside = ((global_rows >= 0) & (global_rows < row_count * slab_count)).astype(jnp.float32)[
        :, None, None
    ]

    def advance(fields, drag_map, forced):
        widened = padded(fields, (("gy", 2),), 2)
        laplace = take_rows(widened, 3, row_count) - 2.0 * fields + take_rows(widened, 1, row_count)
        provisional = fields + DIFFUSION * (laplace - wave_square * fields)
        stream_star = provisional[0] - drag_map(fields[0])
        normal_star = provisional[1]
        if forced:
            normal_star = normal_star + lift_own[:, None, None] * control_hat[:, None]
        provisional = jnp.stack([stream_star, normal_star, provisional[2]])
        normal_wide = widened[1]
        middle = take_rows(normal_wide, 1, row_count + 2)
        near_star = middle + DIFFUSION * (
            take_rows(normal_wide, 2, row_count + 2)
            - 2.0 * middle
            + take_rows(normal_wide, 0, row_count + 2)
            - wave_square * middle
        )
        if forced:
            near_star = near_star + lift_near[:, None, None] * control_hat[:, None]
        near_star = inside * near_star
        normal_slope = 0.5 * (
            take_rows(near_star, 2, row_count) - take_rows(near_star, 0, row_count)
        )
        return (provisional, normal_slope)

    def apply_blocks(values, transposed):
        summed = jnp.zeros_like(values)
        for column in range(row_count):
            if transposed:
                factor = schur_inverse[column][None]
            else:
                factor = schur_inverse[:, column][None]
            summed = summed + factor * values[:, column : column + 1]
        return summed

    def compose(earlier, later):
        return (later[0] * earlier[0], later[1] + later[0][None] * earlier[1])

    def solve(source, transposed):
        last_row = row_count - 1
        if transposed:
            first_column = schur_inverse[0]
            last_column = schur_inverse[last_row]
        else:
            first_column = schur_inverse[:, 0]
            last_column = schur_inverse[:, last_row]
        direct = apply_blocks(source, transposed)
        ratio_term = first_column[last_row]
        offset = direct[:, last_row]
        turn_term = last_column[0]
        neutral = (jnp.ones_like(ratio_term), jnp.zeros_like(offset))
        entering = prefix((ratio_term, offset), "gy", compose, neutral, False)[1]
        partial_value = direct + first_column[None] * entering[:, None]
        leaving = prefix((turn_term, partial_value[:, 0]), "gy", compose, neutral, True)[1]
        return partial_value + last_column[None] * leaving[:, None]

    def project(fields, normal_slope, transposed):
        divergence = rotate(fields[0], stream_factor) + normal_slope + rotate(fields[2], span_wave)
        pressure = solve(divergence, transposed)
        pressure_wide = padded(pressure, (("gy", 1),), 1)
        pressure_slope = 0.5 * (
            take_rows(pressure_wide, 2, row_count) - take_rows(pressure_wide, 0, row_count)
        )
        return jnp.stack(
            [
                fields[0] - rotate(pressure, stream_factor),
                fields[1] - pressure_slope,
                fields[2] - rotate(pressure, span_wave),
            ]
        )

    fields = initial_state
    for section_index in range(STEPS):
        provisional, normal_slope = advance(fields, forward_drag, True)
        fields = project(provisional, normal_slope, False)
    seed_wide = padded(fields[1], (("gy", 1),), 1)
    normal_slope = 0.5 * (take_rows(seed_wide, 2, row_count) - take_rows(seed_wide, 0, row_count))
    costate = fields
    wall_sum = jnp.zeros_like(control_hat)
    for section_index in range(STEPS):
        projected = project(costate, normal_slope, True)
        wall_sum = wall_sum + jnp.sum(lift_own[:, None, None] * projected[1], axis=1)
        if section_index + 1 < STEPS:
            costate, normal_slope = advance(projected, adjoint_drag, False)
    wall_plane = to_physical((wall_sum / mode_weight)[:, None])[0]
    control_gradient = sent_and_summed(wall_plane, "gy", 1)
    return (fields, control_gradient)


def solution(mesh):
    return jax.shard_map(
        per_device,
        mesh=mesh,
        in_specs=(
            P(None, None, "gy", "xz", None),
            P("gy", "xz", None),
            P("xz", None),
            P(),
            P("gy", None, "xz", None),
        ),
        out_specs=(P(None, None, "gy", "xz", None), P("xz", "gy")),
        check_vma=False,
    )
```

profile of v0, /device:TPU:1, one launch (start us, length us, event | category | flops | bytes accessed | tf_op | source)
XLA Modules:
  0.0 766.1 jit_solution(16393079877905711963)
XLA Ops:
  3.8 6.1 collective-permute-start.1
  9.9 9.0 %fusion.76 = f32[1,1,8,512]{3,2,1,0:T(8,128)S(1)} fusion(f32[8,1024]{1,0:T(8,128)S(1)} %copy-done), kind=kOutput, calls=%fused_computation.58 | convolution fusion | flops 58200064 | bytes 49152 | tf_op jit(solution)/shard_map/yzn,nk->yzk/dot_general | solution.py:143
  18.9 9.0 %convolution_bitcast_fusion.2 = f32[1,1,8,512]{3,2,1,0:T(8,128)S(1)} fusion(f32[8,1024]{1,0:T(8,128)S(1)} %copy-done), kind=kOutput, calls=%fused_computation.59 | convolution fusion | flops 58195968 | bytes 49152 | tf_op jit(solution)/shard_map/yzn,nk->yzk/dot_general | solution.py:142
  32.8 11.3 %all-to-all-start.2 = ((f32[64,1,128]{2,1,0:T(1,128)}), f32[64,1,128]{2,1,0:T(1,128)S(1)}, u32[]{:S(2)}, u32[]{:S(2)}) async-start(f32[64,1,128]{2,1,0:T(1,128)} %reshape.466), calls=%async_computation.2 | async-start | bytes 65536 | tf_op jit(solution)/shard_map/all_to_all | solution.py:145
  44.1 4.9 convolution_bitcast_fusion
  49.0 4.9 convolution_bitcast_fusion.1
  64.5 10.8 %all-to-all-start = ((f32[64,1,1024]{2,1,0:T(1,128)}), f32[64,1,1024]{2,1,0:T(1,128)S(1)}, u32[]{:S(2)}, u32[]{:S(2)}) async-start(f32[64,1,1024]{2,1,0:T(1,128)} %reshape.468), calls=%async_computation | async-start | bytes 524288 | tf_op jit(solution)/shard_map/all_to_all | solution.py:155
  77.4 4.6 fusion.93
  82.0 4.6 fusion.97
  93.2 6.6 copy.24
  104.0 9.6 %fusion.13 = f32[8,8,1024]{2,1,0:T(8,128)S(1)} fusion(f32[2,8,512,8]{2,3,1,0:T(8,128)S(1)} %broadcast_multiply_fusion.2), kind=kOutput, calls=%fused_computation.16 | convolution fusion | flops 410517504 | bytes 393216 | tf_op jit(solution)/shard_map/ykz,nk->yzn/dot_general | solution.py:157
  113.6 9.7 %fusion.33 = f32[8,8,1024]{2,1,0:T(8,128)S(1)} fusion(f32[8,8,1024]{2,1,0:T(8,128)S(1)} %copy-done.76, f32[8,8,1024]{2,1,0:T(8,128)S(1)} %fusion.13, f32[2,8,512,8]{2,3,1,0:T(8,128)S(1)} %broadcast_multiply_fusion.2), kind=kOutput, calls=%fused_computation.39 | convolution fusion | flops 410648576 | bytes 917504 | tf_op jit(solution)/shard_map/ykz,nk->yzn/dot_general | solution.py:157
  123.4 9.2 %fusion.60 = f32[1,8,8,512]{3,2,1,0:T(8,128)S(1)} fusion(f32[8,8,1024]{2,1,0:T(8,128)S(1)} %fusion.33), kind=kOutput, calls=%fused_computation.50 | convolution fusion | flops 410550272 | bytes 393216 | tf_op jit(solution)/shard_map/yzn,nk->yzk/dot_general | solution.py:143
  132.6 9.5 %fusion.48 = f32[1,8,8,512]{3,2,1,0:T(8,128)S(1)} fusion(f32[8,8,1024]{2,1,0:T(8,128)S(1)} %fusion.33), kind=kOutput, calls=%fused_computation.46 | convolution fusion | flops 410517504 | bytes 393216 | tf_op jit(solution)/shard_map/yzn,nk->yzk/dot_general | solution.py:142
  150.1 10.1 %all-to-all-start.1 = ((f32[64,1,1024]{2,1,0:T(1,128)}), f32[64,1,1024]{2,1,0:T(1,128)S(1)}, u32[]{:S(2)}, u32[]{:S(2)}) async-start(f32[64,1,1024]{2,1,0:T(1,128)} %reshape.470), calls=%async_computation.1 | async-start | bytes 524288 | tf_op jit(solution)/shard_map/all_to_all | solution.py:145
  161.4 11.9 %all-to-all-done.1 = f32[64,1,1024]{2,1,0:T(1,128)S(1)} async-done(((f32[64,1,1024]{2,1,0:T(1,128)}), f32[64,1,1024]{2,1,0:T(1,128)S(1)}, u32[]{:S(2)}, u32[]{:S(2)}) %all-to-all-start.1) | async-done | bytes 262176 | tf_op jit(solution)/shard_map/all_to_all | solution.py:145
  178.2 6.6 copy.27
  188.8 4.9 fusion.107
  193.7 4.9 fusion.88
  199.9 9.7 %all-to-all-start.3 = ((f32[8,24,512]{2,1,0:T(8,128)}), f32[8,24,512]{2,1,0:T(8,128)S(1)}, u32[]{:S(2)}, u32[]{:S(2)}) async-start(f32[8,24,512]{2,1,0:T(8,128)} %broadcast_in_dim.191), calls=%async_computation.3 | async-start | bytes 786432 | tf_op jit(solution)/shard_map/all_to_all | solution.py:34
  209.6 15.1 %all-to-all-done.3 = f32[8,24,512]{2,1,0:T(8,128)S(1)} async-done(((f32[8,24,512]{2,1,0:T(8,128)}), f32[8,24,512]{2,1,0:T(8,128)S(1)}, u32[]{:S(2)}, u32[]{:S(2)}) %all-to-all-start.3) | async-done | bytes 393248 | tf_op jit(solution)/shard_map/all_to_all | solution.py:34
  230.0 15.0 %all-to-all-done.4 = f32[8,24,512]{2,1,0:T(8,128)S(1)} async-done(((f32[8,24,512]{2,1,0:T(8,128)}), f32[8,24,512]{2,1,0:T(8,128)S(1)}, u32[]{:S(2)}, u32[]{:S(2)}) %all-to-all-start.4) | async-done | bytes 393248 | tf_op jit(solution)/shard_map/all_to_all | solution.py:34
  248.5 4.9 fusion.105
  253.4 4.9 fusion.86
  269.0 5.9 all-to-all-start.5
  277.5 4.9 collective-permute-start.5
  292.9 6.6 copy.33
  303.8 9.6 %fusion.9 = f32[8,8,1024]{2,1,0:T(8,128)S(1)} fusion(f32[2,8,512,8]{2,3,1,0:T(8,128)S(1)} %broadcast_multiply_fusion.1), kind=kOutput, calls=%fused_computation.12 | convolution fusion | flops 410517504 | bytes 393216 | tf_op jit(solution)/shard_map/ykz,nk->yzn/dot_general | solution.py:157
  313.3 9.7 %fusion.39 = f32[8,8,1024]{2,1,0:T(8,128)S(1)} fusion(f32[8,8,1024]{2,1,0:T(8,128)S(1)} %copy-done.77, f32[8,8,1024]{2,1,0:T(8,128)S(1)} %fusion.9, f32[2,8,512,8]{2,3,1,0:T(8,128)S(1)} %broadcast_multiply_fusion.1), kind=kOutput, calls=%fused_computation.41 | convolution fusion | flops 410648576 | bytes 917504 | tf_op jit(solution)/shard_map/ykz,nk->yzn/dot_general | solution.py:157
  323.1 9.2 %fusion.66 = f32[1,8,8,512]{3,2,1,0:T(8,128)S(1)} fusion(f32[8,8,1024]{2,1,0:T(8,128)S(1)} %fusion.39), kind=kOutput, calls=%fused_computation.52 | convolution fusion | flops 410550272 | bytes 393216 | tf_op jit(solution)/shard_map/yzn,nk->yzk/dot_general | solution.py:143
  332.3 9.5 %fusion.51 = f32[1,8,8,512]{3,2,1,0:T(8,128)S(1)} fusion(f32[8,8,1024]{2,1,0:T(8,128)S(1)} %fusion.39), kind=kOutput, calls=%fused_computation.47 | convolution fusion | flops 410517504 | bytes 393216 | tf_op jit(solution)/shard_map/yzn,nk->yzk/dot_general | solution.py:142
  345.4 4.5 reshape.474
  349.9 10.4 %all-to-all-start.6 = ((f32[64,1,1024]{2,1,0:T(1,128)}), f32[64,1,1024]{2,1,0:T(1,128)S(1)}, u32[]{:S(2)}, u32[]{:S(2)}) async-start(f32[64,1,1024]{2,1,0:T(1,128)} %reshape.474), calls=%async_computation.6 | async-start | bytes 524288 | tf_op jit(solution)/shard_map/all_to_all | solution.py:145
  360.6 12.7 %all-to-all-done.6 = f32[64,1,1024]{2,1,0:T(1,128)S(1)} async-done(((f32[64,1,1024]{2,1,0:T(1,128)}), f32[64,1,1024]{2,1,0:T(1,128)S(1)}, u32[]{:S(2)}, u32[]{:S(2)}) %all-to-all-start.6) | async-done | bytes 262176 | tf_op jit(solution)/shard_map/all_to_all | solution.py:145
  378.3 6.6 copy.36
  388.9 4.9 fusion.103
  393.8 4.9 fusion.84
  399.7 20.5 %all_to_all.186 = f32[8,24,512]{2,1,0:T(8,128)S(1)} all-to-all(f32[8,24,512]{2,1,0:T(8,128)S(1)} %broadcast_in_dim.198), channel_id=1, replica_groups=mesh['xz'=64,'gy'=8] {'gy'}, dimensions={0} | all-to-all | bytes 786432 | tf_op jit(solution)/shard_map/all_to_all | solution.py:34
  427.4 11.6 %all-to-all-done.8 = f32[8,24,512]{2,1,0:T(8,128)} async-done(((f32[8,24,512]{2,1,0:T(8,128)}), f32[8,24,512]{2,1,0:T(8,128)}, u32[]{:S(2)}, u32[]{:S(2)}) %all-to-all-start.8) | async-done | bytes 393248 | tf_op jit(solution)/shard_map/all_to_all | solution.py:34
  461.1 15.6 %all_to_all.187 = f32[8,24,512]{2,1,0:T(8,128)S(1)} all-to-all(f32[8,24,512]{2,1,0:T(8,128)S(1)} %broadcast_in_dim.200), channel_id=1, replica_groups=mesh['xz'=64,'gy'=8] {'gy'}, dimensions={0} | all-to-all | bytes 786432 | tf_op jit(solution)/shard_map/all_to_all | solution.py:34
  482.0 10.1 %all-to-all-done.10 = f32[8,24,512]{2,1,0:T(8,128)S(1)} async-done(((f32[8,24,512]{2,1,0:T(8,128)}), f32[8,24,512]{2,1,0:T(8,128)S(1)}, u32[]{:S(2)}, u32[]{:S(2)}) %all-to-all-start.10) | async-done | bytes 393248 | tf_op jit(solution)/shard_map/all_to_all | solution.py:34
  493.7 5.6 fusion.101
  499.4 4.9 fusion.82
  511.3 4.6 reshape.476
  515.9 11.3 %all-to-all-start.11 = ((f32[64,1,1024]{2,1,0:T(1,128)}), f32[64,1,1024]{2,1,0:T(1,128)}, u32[]{:S(2)}, u32[]{:S(2)}) async-start(f32[64,1,1024]{2,1,0:T(1,128)} %reshape.476), calls=%async_computation.11 | async-start | bytes 524288 | tf_op jit(solution)/shard_map/all_to_all | solution.py:155
  530.9 4.9 collective-permute-start.13
  546.4 6.6 copy.39
  557.2 9.6 %fusion.5 = f32[8,8,1024]{2,1,0:T(8,128)S(1)} fusion(f32[2,8,512,8]{2,3,1,0:T(8,128)S(1)} %broadcast_multiply_fusion), kind=kOutput, calls=%fused_computation.8 | convolution fusion | flops 410517504 | bytes 393216 | tf_op jit(solution)/shard_map/ykz,nk->yzn/dot_general | solution.py:157
  566.8 9.7 %fusion.45 = f32[8,8,1024]{2,1,0:T(8,128)S(1)} fusion(f32[8,8,1024]{2,1,0:T(8,128)S(1)} %copy-done.78, f32[8,8,1024]{2,1,0:T(8,128)S(1)} %fusion.5, f32[2,8,512,8]{2,3,1,0:T(8,128)S(1)} %broadcast_multiply_fusion), kind=kOutput, calls=%fused_computation.43 | convolution fusion | flops 410648576 | bytes 917504 | tf_op jit(solution)/shard_map/ykz,nk->yzn/dot_general | solution.py:157
  576.6 9.2 %fusion.72 = f32[1,8,8,512]{3,2,1,0:T(8,128)S(1)} fusion(f32[8,8,1024]{2,1,0:T(8,128)S(1)} %fusion.45), kind=kOutput, calls=%fused_computation.54 | convolution fusion | flops 410550272 | bytes 393216 | tf_op jit(solution)/shard_map/yzn,nk->yzk/dot_general | solution.py:143
  585.8 9.5 %fusion.54 = f32[1,8,8,512]{3,2,1,0:T(8,128)S(1)} fusion(f32[8,8,1024]{2,1,0:T(8,128)S(1)} %fusion.45), kind=kOutput, calls=%fused_computation.48 | convolution fusion | flops 410517504 | bytes 393216 | tf_op jit(solution)/shard_map/yzn,nk->yzk/dot_general | solution.py:142
  603.4 11.9 %all-to-all-start.12 = ((f32[64,1,1024]{2,1,0:T(1,128)}), f32[64,1,1024]{2,1,0:T(1,128)S(1)}, u32[]{:S(2)}, u32[]{:S(2)}) async-start(f32[64,1,1024]{2,1,0:T(1,128)} %reshape.478), calls=%async_computation.12 | async-start | bytes 524288 | tf_op jit(solution)/shard_map/all_to_all | solution.py:145
  617.3 10.9 %all-to-all-done.12 = f32[64,1,1024]{2,1,0:T(1,128)S(1)} async-done(((f32[64,1,1024]{2,1,0:T(1,128)}), f32[64,1,1024]{2,1,0:T(1,128)S(1)}, u32[]{:S(2)}, u32[]{:S(2)}) %all-to-all-start.12) | async-done | bytes 262176 | tf_op jit(solution)/shard_map/all_to_all | solution.py:145
  633.2 6.6 copy.42
  644.5 4.9 fusion.99
  649.5 5.9 fusion.80
  656.3 21.6 %all_to_all.188 = f32[8,24,512]{2,1,0:T(8,128)S(1)} all-to-all(f32[8,24,512]{2,1,0:T(8,128)S(1)} %broadcast_in_dim.204), channel_id=1, replica_groups=mesh['xz'=64,'gy'=8] {'gy'}, dimensions={0} | all-to-all | bytes 786432 | tf_op jit(solution)/shard_map/all_to_all | solution.py:34
  678.5 15.7 %all_to_all.189 = f32[8,24,512]{2,1,0:T(8,128)S(1)} all-to-all(f32[8,24,512]{2,1,0:T(8,128)S(1)} %broadcast_in_dim.205), channel_id=1, replica_groups=mesh['xz'=64,'gy'=8] {'gy'}, dimensions={0} | all-to-all | bytes 786432 | tf_op jit(solution)/shard_map/all_to_all | solution.py:34
  701.2 4.6 fusion.91
  705.8 4.6 fusion.95
  714.1 18.2 %all_to_all.190 = f32[64,1,128]{2,1,0:T(1,128)S(1)} all-to-all(f32[64,1,128]{2,1,0:T(1,128)S(1)} %reshape.480), channel_id=1, replica_groups=mesh['xz'=64,'gy'=8] {'xz'}, dimensions={0} | all-to-all | bytes 65536 | tf_op jit(solution)/shard_map/all_to_all | solution.py:155
  734.4 9.5 %fusion.110 = f32[8,1024]{1,0:T(8,128)S(1)} fusion(f32[2,1,512,8]{2,3,0,1:T(8,128)S(1)} %broadcast_multiply_fusion.3), kind=kOutput, calls=%fused_computation.93 | convolution fusion | flops 58195968 | bytes 49152 | tf_op jit(solution)/shard_map/ykz,nk->yzn/dot_general | solution.py:157
  743.9 10.9 %fusion.75 = f32[8,8,128]{2,1,0:T(8,128)} fusion(f32[8,1024]{1,0:T(8,128)S(1)} %fusion.110, f32[2,1,512,8]{2,3,0,1:T(8,128)S(1)} %broadcast_multiply_fusion.3), kind=kOutput, calls=%fused_computation.56 | convolution fusion | flops 58204160 | bytes 81920 | tf_op jit(solution)/shard_map/ykz,nk->yzn/dot_general | solution.py:157
  759.2 5.9 all-to-all-done.16
  (439 shorter events, 199.4 us)
Async XLA Ops:
  2.5 84.2 %collective-permute-start = (f32[3,2,2,8,512]{4,3,2,1,0:T(8,128)}, f32[3,2,2,8,512]{4,3,2,1,0:T(8,128)}, u32[]{:S(2)}, u32[]{:S(2)}) collective-permute-start(f32[3,2,2,8,512]{4,3,2,1,0:T(8,128)} %get-tuple-element.42), channel_id=1, source_target_pairs={{1,0},{2,1},{3,2},{4,3},{5,4},{6,5},{7,6},{9,8},{10,9},{11,10},{12... | collective-permute-start | bytes 589832 | tf_op jit(solution)/shard_map/ppermute | solution.py:25
  3.8 82.9 %collective-permute-start.1 = (f32[3,2,2,8,512]{4,3,2,1,0:T(8,128)}, f32[3,2,2,8,512]{4,3,2,1,0:T(8,128)}, u32[]{:S(2)}, u32[]{:S(2)}) collective-permute-start(f32[3,2,2,8,512]{4,3,2,1,0:T(8,128)} %get-tuple-element.43), channel_id=1, source_target_pairs={{0,1},{1,2},{2,3},{3,4},{4,5},{5,6},{6,7},{8,9},{9,10},{10,11},{11... | collective-permute-start | bytes 589832 | tf_op jit(solution)/shard_map/ppermute | solution.py:23
  27.9 16.2 %copy-start.2 = (f32[3,2,8,8,512]{4,3,2,1,0:T(8,128)S(1)}, f32[3,2,8,8,512]{4,3,2,1,0:T(8,128)}, u32[]{:S(2)}) copy-start(f32[3,2,8,8,512]{4,3,2,1,0:T(8,128)} %param.5) | copy-start | bytes 2359300
  32.8 31.7 %all-to-all-start.2 = ((f32[64,1,128]{2,1,0:T(1,128)}), f32[64,1,128]{2,1,0:T(1,128)S(1)}, u32[]{:S(2)}, u32[]{:S(2)}) async-start(f32[64,1,128]{2,1,0:T(1,128)} %reshape.466), calls=%async_computation.2 | async-start | bytes 65536 | tf_op jit(solution)/shard_map/all_to_all | solution.py:145
  54.0 249.7 %copy-start.51 = (f32[512]{0:T(512)}, f32[512]{0:T(512)S(1)}, u32[]{:S(2)}) copy-start(f32[512]{0:T(512)S(1)} %fusion.225) | copy-start | bytes 6148
  54.0 344.8 %copy-start.61 = (f32[8]{0:T(128)}, f32[8]{0:T(128)S(1)}, u32[]{:S(2)}) copy-start(f32[8]{0:T(128)S(1)} %get-tuple-element.164) | copy-start | bytes 100
  54.0 344.8 %copy-start.65 = (f32[8]{0:T(128)}, f32[8]{0:T(128)S(1)}, u32[]{:S(2)}) copy-start(f32[8]{0:T(128)S(1)} %get-tuple-element.165) | copy-start | bytes 100
  54.0 306.4 %copy-start.43 = (f32[512]{0:T(512)}, f32[512]{0:T(512)S(1)}, u32[]{:S(2)}) copy-start(f32[512]{0:T(512)S(1)} %fusion.226) | copy-start | bytes 6148
  54.1 306.4 %copy-start.47 = (f32[512]{0:T(512)}, f32[512]{0:T(512)S(1)}, u32[]{:S(2)}) copy-start(f32[512]{0:T(512)S(1)} %fusion.224) | copy-start | bytes 6148
  54.8 144.3 %copy-start.33 = (f32[8,512]{1,0:T(8,128)}, f32[8,512]{1,0:T(8,128)S(1)}, u32[]{:S(2)}) copy-start(f32[8,512]{1,0:T(8,128)S(1)} %get-tuple-element.17) | copy-start | bytes 49156
  54.8 170.4 %copy-start.37 = (f32[8,512]{1,0:T(8,128)}, f32[8,512]{1,0:T(8,128)S(1)}, u32[]{:S(2)}) copy-start(f32[8,512]{1,0:T(8,128)S(1)} %get-tuple-element.16) | copy-start | bytes 49156
  64.3 296.2 %copy-start.69 = (f32[10]{0:T(128)}, f32[10]{0:T(128)S(1)}, u32[]{:S(2)}) copy-start(f32[10]{0:T(128)S(1)} %and_convert_fusion) | copy-start | bytes 124
  64.5 23.8 %all-to-all-start = ((f32[64,1,1024]{2,1,0:T(1,128)}), f32[64,1,1024]{2,1,0:T(1,128)S(1)}, u32[]{:S(2)}, u32[]{:S(2)}) async-start(f32[64,1,1024]{2,1,0:T(1,128)} %reshape.468), calls=%async_computation | async-start | bytes 524288 | tf_op jit(solution)/shard_map/all_to_all | solution.py:155
  150.1 23.1 %all-to-all-start.1 = ((f32[64,1,1024]{2,1,0:T(1,128)}), f32[64,1,1024]{2,1,0:T(1,128)S(1)}, u32[]{:S(2)}, u32[]{:S(2)}) async-start(f32[64,1,1024]{2,1,0:T(1,128)} %reshape.470), calls=%async_computation.1 | async-start | bytes 524288 | tf_op jit(solution)/shard_map/all_to_all | solution.py:145
  199.9 24.8 %all-to-all-start.3 = ((f32[8,24,512]{2,1,0:T(8,128)}), f32[8,24,512]{2,1,0:T(8,128)S(1)}, u32[]{:S(2)}, u32[]{:S(2)}) async-start(f32[8,24,512]{2,1,0:T(8,128)} %broadcast_in_dim.191), calls=%async_computation.3 | async-start | bytes 786432 | tf_op jit(solution)/shard_map/all_to_all | solution.py:34
  209.6 15.4 %copy-start.53 = (pred[8]{0:T(512)(128)(4,1)}, pred[8]{0:T(512)(128)(4,1)S(1)}, u32[]{:S(2)}) copy-start(pred[8]{0:T(512)(128)(4,1)S(1)} %iota_compare_fusion.3) | copy-start | bytes 28
  226.1 18.9 %all-to-all-start.4 = ((f32[8,24,512]{2,1,0:T(8,128)}), f32[8,24,512]{2,1,0:T(8,128)S(1)}, u32[]{:S(2)}, u32[]{:S(2)}) async-start(f32[8,24,512]{2,1,0:T(8,128)} %broadcast_in_dim.196), calls=%async_computation.4 | async-start | bytes 786432 | tf_op jit(solution)/shard_map/all_to_all | solution.py:34
  230.0 46.0 %copy-start.71 = (f32[8]{0:T(128)}, f32[8]{0:T(128)S(1)}, u32[]{:S(2)}) copy-start(f32[8]{0:T(128)S(1)} %slice.1088) | copy-start | bytes 100
  230.0 15.9 %copy-start.57 = (pred[8]{0:T(512)(128)(4,1)}, pred[8]{0:T(512)(128)(4,1)S(1)}, u32[]{:S(2)}) copy-start(pred[8]{0:T(512)(128)(4,1)S(1)} %iota_compare_fusion.2) | copy-start | bytes 28
  258.3 17.7 %collective-permute-start.3 = (f32[2,1,8,512]{3,2,1,0:T(8,128)}, f32[2,1,8,512]{3,2,1,0:T(8,128)S(1)}, u32[]{:S(2)}, u32[]{:S(2)}) collective-permute-start(f32[2,1,8,512]{3,2,1,0:T(8,128)} %get-tuple-element.115), channel_id=1, source_target_pairs={{0,1},{1,2},{2,3},{3,4},{4,5},{5,6},{6,7},{8,9},{9,10},{10,11},{11... | collective-permute-start | bytes 98312 | tf_op jit(solution)/shard_map/ppermute | solution.py:23
  259.6 16.4 %collective-permute-start.2 = (f32[2,1,8,512]{3,2,1,0:T(8,128)}, f32[2,1,8,512]{3,2,1,0:T(8,128)S(1)}, u32[]{:S(2)}, u32[]{:S(2)}) collective-permute-start(f32[2,1,8,512]{3,2,1,0:T(8,128)} %get-tuple-element.114), channel_id=1, source_target_pairs={{1,0},{2,1},{3,2},{4,3},{5,4},{6,5},{7,6},{9,8},{10,9},{11,10},{12... | collective-permute-start | bytes 98312 | tf_op jit(solution)/shard_map/ppermute | solution.py:25
  269.0 19.0 %all-to-all-start.5 = ((f32[64,1,1024]{2,1,0:T(1,128)}), f32[64,1,1024]{2,1,0:T(1,128)S(1)}, u32[]{:S(2)}, u32[]{:S(2)}) async-start(f32[64,1,1024]{2,1,0:T(1,128)} %reshape.472), calls=%async_computation.5 | async-start | bytes 524288 | tf_op jit(solution)/shard_map/all_to_all | solution.py:155
  276.2 9.1 %collective-permute-start.4 = (f32[3,2,2,8,512]{4,3,2,1,0:T(8,128)S(1)}, f32[3,2,2,8,512]{4,3,2,1,0:T(8,128)S(1)}, u32[]{:S(2)}, u32[]{:S(2)}) collective-permute-start(f32[3,2,2,8,512]{4,3,2,1,0:T(8,128)S(1)} %get-tuple-element.37), channel_id=1, source_target_pairs={{1,0},{2,1},{3,2},{4,3},{5,4},{6,5},{7,6},{9,8},{10,9},{11,10},{12... | collective-permute-start | bytes 589832 | tf_op jit(solution)/shard_map/ppermute | solution.py:25
  277.5 8.7 %collective-permute-start.5 = (f32[3,2,2,8,512]{4,3,2,1,0:T(8,128)S(1)}, f32[3,2,2,8,512]{4,3,2,1,0:T(8,128)S(1)}, u32[]{:S(2)}, u32[]{:S(2)}) collective-permute-start(f32[3,2,2,8,512]{4,3,2,1,0:T(8,128)S(1)} %get-tuple-element.36), channel_id=1, source_target_pairs={{0,1},{1,2},{2,3},{3,4},{4,5},{5,6},{6,7},{8,9},{9,10},{10,11},{11... | collective-permute-start | bytes 589832 | tf_op jit(solution)/shard_map/ppermute | solution.py:23
  349.9 23.4 %all-to-all-start.6 = ((f32[64,1,1024]{2,1,0:T(1,128)}), f32[64,1,1024]{2,1,0:T(1,128)S(1)}, u32[]{:S(2)}, u32[]{:S(2)}) async-start(f32[64,1,1024]{2,1,0:T(1,128)} %reshape.474), calls=%async_computation.6 | async-start | bytes 524288 | tf_op jit(solution)/shard_map/all_to_all | solution.py:145
  398.8 50.7 %copy-start.4 = (f32[1,8,8,512]{3,2,1,0:T(8,128)}, f32[1,8,8,512]{3,2,1,0:T(8,128)S(1)}, u32[]{:S(2)}) copy-start(f32[1,8,8,512]{3,2,1,0:T(8,128)S(1)} %get-tuple-element.48) | copy-start | bytes 393220
  398.8 50.7 %copy-start.6 = (f32[1,8,8,512]{3,2,1,0:T(8,128)}, f32[1,8,8,512]{3,2,1,0:T(8,128)S(1)}, u32[]{:S(2)}) copy-start(f32[1,8,8,512]{3,2,1,0:T(8,128)S(1)} %get-tuple-element.49) | copy-start | bytes 393220
  399.0 21.2 %copy-start.54 = (pred[8]{0:T(512)(128)(4,1)S(1)}, pred[8]{0:T(512)(128)(4,1)}, u32[]{:S(2)}) copy-start(pred[8]{0:T(512)(128)(4,1)} %copy-done.53) | copy-start | bytes 28
  399.1 21.4 %copy-start.22 = (f32[2,8,512]{2,1,0:T(8,128)}, f32[2,8,512]{2,1,0:T(8,128)S(1)}, u32[]{:S(2)}) copy-start(f32[2,8,512]{2,1,0:T(8,128)S(1)} %get-tuple-element.107) | copy-start | bytes 98308
  399.6 21.0 %copy-start.38 = (f32[8,512]{1,0:T(8,128)S(1)}, f32[8,512]{1,0:T(8,128)}, u32[]{:S(2)}) copy-start(f32[8,512]{1,0:T(8,128)} %copy-done.37) | copy-start | bytes 49156
  420.6 18.4 %copy-start.58 = (pred[8]{0:T(512)(128)(4,1)S(1)}, pred[8]{0:T(512)(128)(4,1)}, u32[]{:S(2)}) copy-start(pred[8]{0:T(512)(128)(4,1)} %copy-done.57) | copy-start | bytes 28
  421.5 17.5 %all-to-all-start.8 = ((f32[8,24,512]{2,1,0:T(8,128)}), f32[8,24,512]{2,1,0:T(8,128)}, u32[]{:S(2)}, u32[]{:S(2)}) async-start(f32[8,24,512]{2,1,0:T(8,128)} %broadcast_in_dim.199), calls=%async_computation.8 | async-start | bytes 786432 | tf_op jit(solution)/shard_map/all_to_all | solution.py:34
  446.8 2.8 collective-permute-start.7
  448.1 4.7 collective-permute-start.6
  452.9 4.4 collective-permute-start.9
  456.0 4.7 collective-permute-start.8
  460.6 16.0 %copy-start.55 = (pred[8]{0:T(512)(128)(4,1)S(1)}, pred[8]{0:T(512)(128)(4,1)}, u32[]{:S(2)}) copy-start(pred[8]{0:T(512)(128)(4,1)} %copy-done.53) | copy-start | bytes 28
  460.8 16.2 %copy-start.23 = (f32[2,8,512]{2,1,0:T(8,128)}, f32[2,8,512]{2,1,0:T(8,128)S(1)}, u32[]{:S(2)}) copy-start(f32[2,8,512]{2,1,0:T(8,128)S(1)} %get-tuple-element.82) | copy-start | bytes 98308
  460.8 16.2 %copy-start.25 = (f32[2,8,512]{2,1,0:T(8,128)}, f32[2,8,512]{2,1,0:T(8,128)S(1)}, u32[]{:S(2)}) copy-start(f32[2,8,512]{2,1,0:T(8,128)S(1)} %get-tuple-element.83) | copy-start | bytes 98308
  460.8 16.2 %copy-start.27 = (f32[2,8,512]{2,1,0:T(8,128)}, f32[2,8,512]{2,1,0:T(8,128)S(1)}, u32[]{:S(2)}) copy-start(f32[2,8,512]{2,1,0:T(8,128)S(1)} %get-tuple-element.84) | copy-start | bytes 98308
  460.8 16.2 %copy-start.29 = (f32[2,8,512]{2,1,0:T(8,128)}, f32[2,8,512]{2,1,0:T(8,128)S(1)}, u32[]{:S(2)}) copy-start(f32[2,8,512]{2,1,0:T(8,128)S(1)} %get-tuple-element.85) | copy-start | bytes 98308
  461.1 16.1 %copy-start.35 = (f32[8,512]{1,0:T(8,128)S(1)}, f32[8,512]{1,0:T(8,128)}, u32[]{:S(2)}) copy-start(f32[8,512]{1,0:T(8,128)} %copy-done.33) | copy-start | bytes 49156
  476.8 15.4 %copy-start.59 = (pred[8]{0:T(512)(128)(4,1)S(1)}, pred[8]{0:T(512)(128)(4,1)}, u32[]{:S(2)}) copy-start(pred[8]{0:T(512)(128)(4,1)} %copy-done.57) | copy-start | bytes 28
  477.2 15.4 %copy-start.24 = (f32[2,8,512]{2,1,0:T(8,128)S(1)}, f32[2,8,512]{2,1,0:T(8,128)}, u32[]{:S(2)}) copy-start(f32[2,8,512]{2,1,0:T(8,128)} %copy-done.23) | copy-start | bytes 98308
  477.2 15.4 %copy-start.26 = (f32[2,8,512]{2,1,0:T(8,128)S(1)}, f32[2,8,512]{2,1,0:T(8,128)}, u32[]{:S(2)}) copy-start(f32[2,8,512]{2,1,0:T(8,128)} %copy-done.25) | copy-start | bytes 98308
  477.2 15.4 %copy-start.28 = (f32[2,8,512]{2,1,0:T(8,128)S(1)}, f32[2,8,512]{2,1,0:T(8,128)}, u32[]{:S(2)}) copy-start(f32[2,8,512]{2,1,0:T(8,128)} %copy-done.27) | copy-start | bytes 98308
  478.0 14.1 %all-to-all-start.10 = ((f32[8,24,512]{2,1,0:T(8,128)}), f32[8,24,512]{2,1,0:T(8,128)S(1)}, u32[]{:S(2)}, u32[]{:S(2)}) async-start(f32[8,24,512]{2,1,0:T(8,128)} %broadcast_in_dim.201), calls=%async_computation.10 | async-start | bytes 786432 | tf_op jit(solution)/shard_map/all_to_all | solution.py:34
  504.2 25.2 %collective-permute-start.11 = (f32[2,1,8,512]{3,2,1,0:T(8,128)S(1)}, f32[2,1,8,512]{3,2,1,0:T(8,128)S(1)}, u32[]{:S(2)}, u32[]{:S(2)}) collective-permute-start(f32[2,1,8,512]{3,2,1,0:T(8,128)S(1)} %get-tuple-element.71), channel_id=1, source_target_pairs={{0,1},{1,2},{2,3},{3,4},{4,5},{5,6},{6,7},{8,9},{9,10},{10,11},{11... | collective-permute-start | bytes 98312 | tf_op jit(solution)/shard_map/ppermute | solution.py:23
  506.5 23.0 %collective-permute-start.10 = (f32[2,1,8,512]{3,2,1,0:T(8,128)S(1)}, f32[2,1,8,512]{3,2,1,0:T(8,128)S(1)}, u32[]{:S(2)}, u32[]{:S(2)}) collective-permute-start(f32[2,1,8,512]{3,2,1,0:T(8,128)S(1)} %get-tuple-element.70), channel_id=1, source_target_pairs={{1,0},{2,1},{3,2},{4,3},{5,4},{6,5},{7,6},{9,8},{10,9},{11,10},{12... | collective-permute-start | bytes 98312 | tf_op jit(solution)/shard_map/ppermute | solution.py:25
  511.3 15.9 %copy-start.5 = (f32[1,8,8,512]{3,2,1,0:T(8,128)S(1)}, f32[1,8,8,512]{3,2,1,0:T(8,128)}, u32[]{:S(2)}) copy-start(f32[1,8,8,512]{3,2,1,0:T(8,128)} %copy-done.4) | copy-start | bytes 393220
  511.3 15.9 %copy-start.7 = (f32[1,8,8,512]{3,2,1,0:T(8,128)S(1)}, f32[1,8,8,512]{3,2,1,0:T(8,128)}, u32[]{:S(2)}) copy-start(f32[1,8,8,512]{3,2,1,0:T(8,128)} %copy-done.6) | copy-start | bytes 393220
  511.3 15.9 %copy-start.9 = (f32[1,8,8,512]{3,2,1,0:T(8,128)S(1)}, f32[1,8,8,512]{3,2,1,0:T(8,128)}, u32[]{:S(2)}) copy-start(f32[1,8,8,512]{3,2,1,0:T(8,128)} %copy-done.8) | copy-start | bytes 393220
  511.3 15.9 %copy-start.11 = (f32[1,8,8,512]{3,2,1,0:T(8,128)S(1)}, f32[1,8,8,512]{3,2,1,0:T(8,128)}, u32[]{:S(2)}) copy-start(f32[1,8,8,512]{3,2,1,0:T(8,128)} %copy-done.10) | copy-start | bytes 393220
  515.9 24.6 %all-to-all-start.11 = ((f32[64,1,1024]{2,1,0:T(1,128)}), f32[64,1,1024]{2,1,0:T(1,128)}, u32[]{:S(2)}, u32[]{:S(2)}) async-start(f32[64,1,1024]{2,1,0:T(1,128)} %reshape.476), calls=%async_computation.11 | async-start | bytes 524288 | tf_op jit(solution)/shard_map/all_to_all | solution.py:155
  529.6 9.0 %collective-permute-start.12 = (f32[3,2,2,8,512]{4,3,2,1,0:T(8,128)S(1)}, f32[3,2,2,8,512]{4,3,2,1,0:T(8,128)S(1)}, u32[]{:S(2)}, u32[]{:S(2)}) collective-permute-start(f32[3,2,2,8,512]{4,3,2,1,0:T(8,128)S(1)} %get-tuple-element.29), channel_id=1, source_target_pairs={{1,0},{2,1},{3,2},{4,3},{5,4},{6,5},{7,6},{9,8},{10,9},{11,10},{12... | collective-permute-start | bytes 589832 | tf_op jit(solution)/shard_map/ppermute | solution.py:25
  530.9 8.5 %collective-permute-start.13 = (f32[3,2,2,8,512]{4,3,2,1,0:T(8,128)S(1)}, f32[3,2,2,8,512]{4,3,2,1,0:T(8,128)S(1)}, u32[]{:S(2)}, u32[]{:S(2)}) collective-permute-start(f32[3,2,2,8,512]{4,3,2,1,0:T(8,128)S(1)} %get-tuple-element.28), channel_id=1, source_target_pairs={{0,1},{1,2},{2,3},{3,4},{4,5},{5,6},{6,7},{8,9},{9,10},{10,11},{11... | collective-permute-start | bytes 589832 | tf_op jit(solution)/shard_map/ppermute | solution.py:23
  603.4 24.9 %all-to-all-start.12 = ((f32[64,1,1024]{2,1,0:T(1,128)}), f32[64,1,1024]{2,1,0:T(1,128)S(1)}, u32[]{:S(2)}, u32[]{:S(2)}) async-start(f32[64,1,1024]{2,1,0:T(1,128)} %reshape.478), calls=%async_computation.12 | async-start | bytes 524288 | tf_op jit(solution)/shard_map/all_to_all | solution.py:145
  655.7 22.2 %copy-start.56 = (pred[8]{0:T(512)(128)(4,1)S(1)}, pred[8]{0:T(512)(128)(4,1)}, u32[]{:S(2)}) copy-start(pred[8]{0:T(512)(128)(4,1)} %copy-done.53) | copy-start | bytes 28
  656.3 22.1 %copy-start.36 = (f32[8,512]{1,0:T(8,128)S(1)}, f32[8,512]{1,0:T(8,128)}, u32[]{:S(2)}) copy-start(f32[8,512]{1,0:T(8,128)} %copy-done.33) | copy-start | bytes 49156
  678.0 16.2 %copy-start.60 = (pred[8]{0:T(512)(128)(4,1)S(1)}, pred[8]{0:T(512)(128)(4,1)}, u32[]{:S(2)}) copy-start(pred[8]{0:T(512)(128)(4,1)} %copy-done.57) | copy-start | bytes 28
  694.8 2.9 collective-permute-start.15
  696.4 4.7 collective-permute-start.14
  743.9 21.8 %copy-start.1 = (f32[8,1024]{1,0:T(8,128)S(1)}, f32[8,1024]{1,0:T(8,128)}, u32[]{:S(2)}) copy-start(f32[8,1024]{1,0:T(8,128)} %param.7) | copy-start | bytes 98308
  754.9 10.2 %all-to-all-start.16 = ((f32[8,8,128]{2,1,0:T(8,128)}), f32[8,8,128]{2,1,0:T(8,128)S(1)}, u32[]{:S(2)}, u32[]{:S(2)}) async-start(f32[8,8,128]{2,1,0:T(8,128)} %fusion.75), calls=%async_computation.16 | async-start | bytes 65536 | tf_op jit(solution)/shard_map/all_to_all | solution.py:99
  (44 other events, 318.6 us)
where the time goes:
time: 778 us; the launch traced here: 766 us
  matrix products  232 us (30%)
  local copies, waits for them, and re-layouts  155 us (20%)
  starting transfers between devices  132 us (17%)
  waiting for transfers between devices  112 us (14%)
  blocking collectives  91.5 us (12%)
  other arithmetic  39.9 us (5%)
    all_to_all x4, blocking collectives, copy_for_each(): return lax.all_to_all(copies, axis, split_axis=0, concat_axis=0, tiled=True)  73.4 us
    unnamed x176, local copies, waits for them, and re-layouts  55 us
    all_to_all x4, waiting for transfers between devices, copy_for_each(): return lax.all_to_all(copies, axis, split_axis=0, concat_axis=0, tiled=True)  51.8 us
    all_to_all x4, starting transfers between devices, to_spectral(): lax.all_to_all(halfway, 'xz', split_axis=3, concat_axis=2, tiled=True)  43.8 us
    dot_general x4, matrix products, to_physical(): jnp.einsum('ykz,nk->yzn', weighted[1], sin_x, precision=HIGHEST)  39.7 us
    dot_general x4, matrix products, to_physical(): jnp.einsum('ykz,nk->yzn', weighted[0], cos_x, precision=HIGHEST)  38.8 us
    dot_general x4, matrix products, to_spectral(): real_half = jnp.einsum('yzn,nk->yzk', physical, cos_x, precision=HIGHEST)  37.6 us
    dot_general x4, matrix products, to_spectral(): imag_half = -jnp.einsum('yzn,nk->yzk', physical, sin_x, precision=HIGHEST)  36.6 us
  transfers between devices with their start and end apart: 28, of which 17 were waited for; matrix products, arithmetic and copies ran while one was open for 11% of the time, Pallas kernels for 0%

commit v1 on v0

v1 whole, which is shorter than its diff:
```python
import functools
import math

import jax
import jax.numpy as jnp
import numpy as np
from jax import lax
from jax.experimental import pallas as pl
from jax.experimental.pallas import tpu as pltpu
from jax.sharding import PartitionSpec as P

MESH = pl.DeviceIdType.MESH
F32 = jnp.float32
BF16 = jnp.bfloat16
DIFFUSION = 0.04
NX = 1024
NZ = 512
KX = 512
ROWS = 8
MODES = 8
PEERS = 64
SLABS = 8
ROUNDS = 4
CONTROL_SLOT = 6
FINAL_SLOT = 7


def base_table(period, scale):
    k = np.arange(512)
    high = 2.0 * np.pi * ((32 * np.arange(16)[:, None] * k) % period) / period
    low = 2.0 * np.pi * ((np.arange(32)[:, None] * k) % period) / period
    return np.concatenate(
        [np.cos(high), np.sin(high), np.cos(low) * scale, np.sin(low) * scale]
    ).astype(np.float32)


def split(x):
    hi = x.astype(BF16)
    return hi, (x - hi.astype(F32))


def butterfly(tiles, lane):
    tiles = list(tiles)
    for bit in range(4):
        step = 1 << bit
        shift = 8 * step
        upper = (lane // shift) % 2 == 1
        for a in range(16):
            if a & step == 0:
                x, y = tiles[a], tiles[a | step]
                tiles[a] = jnp.where(upper, pltpu.roll(y, shift, 1), x)
                tiles[a | step] = jnp.where(upper, y, pltpu.roll(x, 128 - shift, 1))
    return tiles


def kernel(
    state_in, drag_in, ctrl_in, lift_ref, schur, base_x, base_z,
    out_state, out_grad,
    st, pu, pv, pw, divb, direct, pbuf, wall, chat, zin, zout,
    tx, tzh, tzl, dg, waves, amat,
    send, recv, hsend, hrecv, ssend, srecv, gsend, grecv, fsend, frecv,
    send_sem, recv_sem, hsend_sem, hrecv_sem, ssend_sem, srecv_sem, misc_sem,
):
    me = lax.axis_index("xz")
    slab = lax.axis_index("gy")
    barrier = pltpu.get_barrier_semaphore()

    @pl.loop(1, PEERS)
    def _(i):
        pl.semaphore_signal(
            barrier, inc=1, device_id=(lax.rem(me + i, PEERS), slab), device_id_type=MESH
        )

    @pl.loop(1, SLABS)
    def _(i):
        pl.semaphore_signal(
            barrier, inc=1, device_id=(me, lax.rem(slab + i, SLABS)), device_id_type=MESH
        )

    lane = lax.broadcasted_iota(jnp.int32, (8, 128), 1)
    wide_lane = lax.broadcasted_iota(jnp.int32, (KX, 128), 1)
    left = wide_lane < 64
    odd = lax.broadcasted_iota(jnp.int32, (KX, 128), 0) % 2 == 1

    mode = me * MODES + lax.broadcasted_iota(jnp.int32, (MODES, NZ), 0)
    span = lax.broadcasted_iota(jnp.int32, (MODES, NZ), 1)
    kx = (2.0 * math.pi / NX) * mode.astype(F32)
    signed = jnp.where(span < NZ // 2, span, span - NZ)
    kz = jnp.where(span == NZ // 2, 0.0, (2.0 * math.pi / NZ) * signed.astype(F32))
    waves[0] = kx
    waves[1] = kz
    waves[2] = kx * kx + kz * kz
    waves[3] = jnp.where(mode == 0, 1.0, 2.0).astype(F32)

    @pl.loop(0, 16)
    def _(i):
        rows = pl.ds(pl.multiple_of(i * 32, 32), 32)
        for base, which in ((base_x, 0), (base_z, 1)):
            ca = base[pl.ds(i, 1), :]
            sa = base[pl.ds(16 + i, 1), :]
            cb = base[32:64, :]
            sb = base[64:96, :]
            c_hi, c_lo = split(ca * cb - sa * sb)
            s_hi, s_lo = split(sa * cb + ca * sb)
            if which == 0:
                tx[rows, 0:512] = c_hi
                tx[rows, 512:1024] = c_lo.astype(BF16)
                tx[rows, 1024:1536] = s_hi
                tx[rows, 1536:2048] = s_lo.astype(BF16)
            else:
                tzh[rows, 0:512] = c_hi
                tzh[rows, 512:1024] = s_hi
                tzl[rows, 0:512] = c_lo.astype(BF16)
                tzl[rows, 512:1024] = s_lo.astype(BF16)

    for b in range(4):
        lo = drag_in[:, :, 128 * b : 128 * b + 128].reshape(64, 128)
        hi = drag_in[:, :, 512 + 128 * b : 640 + 128 * b].reshape(64, 128)
        dg[128 * b : 128 * b + 128, :] = jnp.concatenate([lo, hi], axis=0).T

    for comp in range(3):
        for c in range(2):
            @pl.loop(0, ROWS)
            def _(y):
                st[comp, y + 2, c] = state_in[comp, c, y]

    gsend[0] = schur[0, 0]
    gsend[1] = schur[0, 7]
    gsend[2] = schur[7, 0]
    gsend[3] = schur[7, 7]

    def x_inverse(slot):
        value = recv[slot].reshape(KX, 128)
        hi = value.astype(BF16).astype(F32)
        lo = value - hi
        real = jnp.where(left, hi, pltpu.roll(lo, 64, 1))
        imag = -jnp.where(left, pltpu.roll(hi, 64, 1), lo)
        rc = jnp.concatenate([real, jnp.where(odd, -real, real)], axis=1).astype(BF16)
        rs = jnp.concatenate([imag, jnp.where(odd, -imag, imag)], axis=1).astype(BF16)
        out = jnp.dot(tx[:, 0:512], rc, preferred_element_type=F32)
        out += jnp.dot(tx[:, 512:1024], rc, preferred_element_type=F32)
        out += jnp.dot(tx[:, 1024:1536], rs, preferred_element_type=F32)
        out += jnp.dot(tx[:, 1536:2048], rs, preferred_element_type=F32)
        near, far = out[:, 0:128], out[:, 128:256]
        near = near + pltpu.roll(near, 64, 1)
        far = far + pltpu.roll(far, 64, 1)
        return jnp.where(left, near, far)

    def x_forward(value, slot):
        turned = pltpu.roll(value, 64, 1)
        total = value + turned
        gap = jnp.where(left, value - turned, turned - value)

        def packed(part):
            hi = part.astype(BF16).astype(F32)
            return jnp.where(left, hi, part - hi)

        ra = jnp.concatenate([packed(total), packed(gap)], axis=1).astype(BF16)
        with_cos = jnp.dot(tx[:, 0:512], ra, preferred_element_type=F32)
        with_cos += jnp.dot(tx[:, 512:1024], ra, preferred_element_type=F32)
        with_sin = jnp.dot(tx[:, 1024:1536], ra, preferred_element_type=F32)
        with_sin += jnp.dot(tx[:, 1536:2048], ra, preferred_element_type=F32)

        def folded(part):
            part = jnp.where(odd, part[:, 128:256], part[:, 0:128])
            return part + pltpu.roll(part, 64, 1)

        result = jnp.where(left, folded(with_cos), -folded(with_sin))
        send[slot] = result.reshape(PEERS, 8, 128)

    def z_dot(value):
        hi, lo = split(value)
        both = jnp.concatenate([hi, lo.astype(BF16)], axis=0)
        out = jnp.dot(both, tzh[...], preferred_element_type=F32)
        out = out[0:128] + out[128:256]
        out += jnp.dot(hi, tzl[...], preferred_element_type=F32)
        out = out.reshape(ROWS, 2, MODES, 1024)
        return out[:, :, :, 0:512], out[:, :, :, 512:1024]

    def z_inverse(value, slot):
        with_cos, with_sin = z_dot(value)
        zout[:, 0] = with_cos[:, 0] - with_sin[:, 1]
        zout[:, 1] = with_sin[:, 0] + with_cos[:, 1]

        @pl.loop(0, 4)
        def _(j):
            lanes = pl.ds(pl.multiple_of(j * 128, 128), 128)
            tiles = [zout[a % 8, a // 8, :, lanes] for a in range(16)]
            for g, tile in enumerate(butterfly(tiles, lane)):
                send[slot, j * 16 + g] = tile

    def z_forward(slot):
        @pl.loop(0, 4)
        def _(j):
            lanes = pl.ds(pl.multiple_of(j * 128, 128), 128)
            tiles = [recv[slot, j * 16 + g] for g in range(16)]
            for a, tile in enumerate(butterfly(tiles, lane)):
                zin[a % 8, a // 8, :, lanes] = tile

        with_cos, with_sin = z_dot(zin[...].reshape(128, NZ))
        zout[:, 0] = with_cos[:, 0] + with_sin[:, 1]
        zout[:, 1] = with_cos[:, 1] - with_sin[:, 0]

    def exchange(slot):
        @pl.loop(1, PEERS)
        def _(i):
            peer = lax.rem(me + i, PEERS)
            pltpu.make_async_remote_copy(
                src_ref=send.at[slot, peer],
                dst_ref=recv.at[slot, me],
                send_sem=send_sem.at[slot],
                recv_sem=recv_sem.at[slot],
                device_id=(peer, slab),
                device_id_type=MESH,
            ).start()

        recv[slot, me] = send[slot, me]

    def arrived(slot):
        whole = recv.at[slot, pl.ds(0, PEERS - 1)]
        pltpu.make_async_copy(whole, whole, recv_sem.at[slot]).wait()

    def left_device(buffer, sem, count):
        whole = buffer.at[pl.ds(0, count)]
        pltpu.make_async_copy(whole, whole, sem).wait()

    def to_slabs(source, target, out_sem, in_sem):
        @pl.loop(1, SLABS)
        def _(i):
            peer = lax.rem(slab + i, SLABS)
            pltpu.make_async_remote_copy(
                src_ref=source(peer),
                dst_ref=target,
                send_sem=out_sem,
                recv_sem=in_sem,
                device_id=(me, peer),
                device_id_type=MESH,
            ).start()

    for b in range(4):
        near = ctrl_in[:, 128 * b : 128 * b + 128]
        far = ctrl_in[:, 512 + 128 * b : 640 + 128 * b]
        blank = jnp.zeros((56, 128), F32)
        pieces = jnp.concatenate([near, blank, far, blank], axis=0)
        zin_rows = pieces.T
        wall_rows = pl.ds(128 * b, 128)
        send[FINAL_SLOT, 16 * b : 16 * b + 16] = zin_rows.reshape(16, 8, 128)
        del wall_rows
    x_forward(send[FINAL_SLOT].reshape(KX, 128), CONTROL_SLOT)

    pl.semaphore_wait(barrier, PEERS - 1 + SLABS - 1)

    to_slabs(lambda peer: gsend, grecv.at[slab], misc_sem.at[0], misc_sem.at[1])
    wall[...] = jnp.zeros_like(wall)

    @pl.loop(0, ROUNDS)
    def _(r):
        adjoint = r // 2
        moving = r != 2
        rate = jnp.where(moving, DIFFUSION, 0.0).astype(F32)

        @pl.when(moving)
        def _():
            before = jnp.where(r < 2, waves[3], 1.0)
            z_inverse((st[0, 2:10] * before).reshape(128, NZ), 2 * jnp.where(r == 3, 2, r))

        for side, (u_row, v_row) in enumerate(((9, 8), (2, 2))):
            hsend[r, side, 0] = st[0, u_row]
            hsend[r, side, 1] = st[1, v_row]
            hsend[r, side, 2] = st[1, v_row + 1]
            hsend[r, side, 3] = st[2, u_row]
        for side in range(2):
            peer = lax.rem(slab + (1 if side == 0 else SLABS - 1), SLABS)
            pltpu.make_async_remote_copy(
                src_ref=hsend.at[r, side],
                dst_ref=hrecv.at[r, side],
                send_sem=hsend_sem.at[r, side],
                recv_sem=hrecv_sem.at[r, side],
                device_id=(me, peer),
                device_id_type=MESH,
            ).start()

        @pl.when(moving)
        def _():
            exchange(2 * jnp.where(r == 3, 2, r))

        @pl.when(r == 0)
        def _():
            exchange(CONTROL_SLOT)

        for side in range(2):
            whole = hrecv.at[r, side]
            pltpu.make_async_copy(whole, whole, hrecv_sem.at[r, side]).wait()
        for side, (u_row, v_row, edge) in enumerate(((1, 0, 0), (10, 10, SLABS - 1))):
            open_side = slab != edge
            st[0, u_row] = jnp.where(open_side, hrecv[r, side, 0], 0.0)
            st[1, v_row] = jnp.where(open_side, hrecv[r, side, 1], 0.0)
            st[1, v_row + 1] = jnp.where(open_side, hrecv[r, side, 2], 0.0)
            st[2, u_row] = jnp.where(open_side, hrecv[r, side, 3], 0.0)

        square = waves[2]

        def diffused(comp, row):
            middle = st[comp, row]
            around = st[comp, row + 1] - 2.0 * middle + st[comp, row - 1]
            return middle + rate * (around - square * middle)

        @pl.loop(0, ROWS)
        def _(y):
            pu[y] = diffused(0, y + 2)
            pw[y] = diffused(2, y + 2)

        @pl.loop(0, ROWS + 2)
        def _(y):
            row = slab * ROWS + y - 1
            inside = jnp.logical_and(row >= 0, row < ROWS * SLABS)
            pv[y] = jnp.where(inside, diffused(1, y + 1), 0.0)

        @pl.when(moving)
        def _():
            slot = 2 * jnp.where(r == 3, 2, r)
            arrived(slot)
            x_forward(x_inverse(slot) * dg[...], slot + 1)
            exchange(slot + 1)

        @pl.when(r == 0)
        def _():
            arrived(CONTROL_SLOT)
            z_forward(CONTROL_SLOT)
            chat[...] = zout[0]
            pltpu.make_async_copy(
                grecv.at[pl.ds(0, SLABS - 1)], grecv.at[pl.ds(0, SLABS - 1)], misc_sem.at[1]
            ).wait()

            def gather_a(i, a):
                b = SLABS - 1 - i
                return grecv[b, 0] + grecv[b, 1] * a * grecv[b, 2]

            amat[...] = lax.fori_loop(0, SLABS - 1 - slab, gather_a, jnp.zeros((MODES, NZ), F32))

        @pl.when(r < 2)
        def _():
            @pl.loop(0, ROWS + 2)
            def _(y):
                row = slab * ROWS + y - 1
                inside = jnp.logical_and(row >= 0, row < ROWS * SLABS)
                safe = jnp.clip(row, 0, ROWS * SLABS - 1)
                level = jnp.where(inside, lift_ref[safe], 0.0)
                pv[y] = pv[y] + level * chat[...]

        kxv, kzv = waves[0], waves[1]

        @pl.when(moving)
        def _():
            slot = 2 * jnp.where(r == 3, 2, r) + 1
            arrived(slot)
            z_forward(slot)
            after = jnp.where(r < 2, 1.0, waves[3])

            @pl.loop(0, ROWS)
            def _(y):
                pu[y] = pu[y] - zout[y] * after

        @pl.loop(0, ROWS)
        def _(y):
            slope = 0.5 * (pv[y + 2] - pv[y])
            divb[y, 0] = slope[0] - kxv * pu[y, 1] - kzv * pw[y, 1]
            divb[y, 1] = slope[1] + kxv * pu[y, 0] + kzv * pw[y, 0]

        def entry(i, j):
            return schur[i + adjoint * (j - i), j + adjoint * (i - j)]

        @pl.loop(0, ROWS)
        def _(i):
            total = entry(i, 0) * divb[0]
            for j in range(1, ROWS):
                total = total + entry(i, j) * divb[j]
            direct[i] = total

        ratio = entry(7, 0)
        turn = entry(0, 7)
        last = direct[7]
        ssend[r, 0] = last
        ssend[r, 1] = direct[0] + turn * (amat[...] * last)
        to_slabs(
            lambda peer: ssend.at[r, jnp.where(peer > slab, 0, 1)],
            srecv.at[r, slab],
            ssend_sem.at[r],
            srecv_sem.at[r],
        )
        whole = srecv.at[r, pl.ds(0, SLABS - 1)]
        pltpu.make_async_copy(whole, whole, srecv_sem.at[r]).wait()

        blank = jnp.zeros((2, MODES, NZ), F32)
        entering = lax.fori_loop(
            0, slab, lambda b, z: srecv[r, b] + grecv[b, 2 - adjoint] * z, blank
        )

        def suffix(i, e):
            b = SLABS - 1 - i
            return srecv[r, b] + grecv[b, 1 + adjoint] * e

        above = lax.fori_loop(0, SLABS - 1 - slab, suffix, blank)
        leaving = above + amat[...] * (last + ratio * entering)
        pbuf[9] = leaving

        @pl.loop(0, ROWS)
        def _(i):
            pbuf[i + 1] = direct[i] + entry(i, 0) * entering + entry(i, 7) * leaving

        below = grecv[lax.max(slab - 1, 0), 3]
        pbuf[0] = jnp.where(slab == 0, 0.0, entering + below * pbuf[1])

        @pl.loop(0, ROWS)
        def _(y):
            p0, p1 = pbuf[y + 1, 0], pbuf[y + 1, 1]
            st[0, y + 2, 0] = pu[y, 0] + kxv * p1
            st[0, y + 2, 1] = pu[y, 1] - kxv * p0
            st[2, y + 2, 0] = pw[y, 0] + kzv * p1
            st[2, y + 2, 1] = pw[y, 1] - kzv * p0
            normal = pv[y + 1] - 0.5 * (pbuf[y + 2] - pbuf[y])
            st[1, y + 2] = normal
            level = jnp.where(r >= 2, lift_ref[slab * ROWS + y], 0.0)
            wall[...] = wall[...] + level * normal

        @pl.when(r == 1)
        def _():
            @pl.loop(0, ROWS)
            def _(y):
                for comp in range(3):
                    for c in range(2):
                        out_state[comp, c, y] = st[comp, y + 2, c]

    zin[...] = jnp.zeros_like(zin)
    zin[0] = wall[...]
    z_inverse(zin[...].reshape(128, NZ), FINAL_SLOT)
    exchange(FINAL_SLOT)
    arrived(FINAL_SLOT)
    plane = x_inverse(FINAL_SLOT)
    for b in range(4):
        turned = plane[128 * b : 128 * b + 128, :].T
        fsend[b] = turned[0:8]
        fsend[4 + b] = turned[64:72]
    to_slabs(
        lambda peer: fsend.at[peer], frecv.at[slab], misc_sem.at[2], misc_sem.at[3]
    )
    frecv[slab] = fsend[slab]
    left_device(frecv, misc_sem.at[3], SLABS - 1)
    total = frecv[0]
    for b in range(1, SLABS):
        total = total + frecv[b]
    out_grad[...] = total

    @pl.loop(0, 8)
    def _(slot):
        left_device(send.at[slot], send_sem.at[slot], PEERS - 1)

    @pl.loop(0, ROUNDS)
    def _(r):
        for side in range(2):
            whole = hsend.at[r, side]
            pltpu.make_async_copy(whole, whole, hsend_sem.at[r, side]).wait()
        left_device(srecv.at[r], ssend_sem.at[r], SLABS - 1)

    left_device(grecv, misc_sem.at[0], SLABS - 1)
    left_device(frecv, misc_sem.at[2], SLABS - 1)


def per_device(initial_state, drag_rate, wall_control, lift_profile, schur_inverse):
    row = (2, MODES, NZ)
    vmem = pl.BlockSpec(memory_space=pltpu.VMEM)
    smem = pl.BlockSpec(memory_space=pltpu.SMEM)
    dma = pltpu.SemaphoreType.DMA
    return pl.pallas_call(
        kernel,
        out_shape=(
            jax.ShapeDtypeStruct((3, 2, ROWS, MODES, NZ), F32),
            jax.ShapeDtypeStruct((8, 128), F32),
        ),
        in_specs=[vmem, vmem, vmem, smem, vmem, vmem, vmem],
        out_specs=(vmem, vmem),
        scratch_shapes=[
            pltpu.VMEM((3, ROWS + 4, *row), F32),
            pltpu.VMEM((ROWS, *row), F32),
            pltpu.VMEM((ROWS + 2, *row), F32),
            pltpu.VMEM((ROWS, *row), F32),
            pltpu.VMEM((ROWS, *row), F32),
            pltpu.VMEM((ROWS, *row), F32),
            pltpu.VMEM((ROWS + 2, *row), F32),
            pltpu.VMEM(row, F32),
            pltpu.VMEM(row, F32),
            pltpu.VMEM((ROWS, *row), F32),
            pltpu.VMEM((ROWS, *row), F32),
            pltpu.VMEM((512, 2048), BF16),
            pltpu.VMEM((512, 1024), BF16),
            pltpu.VMEM((512, 1024), BF16),
            pltpu.VMEM((512, 128), F32),
            pltpu.VMEM((4, MODES, NZ), F32),
            pltpu.VMEM((MODES, NZ), F32),
            pltpu.VMEM((8, PEERS, 8, 128), F32),
            pltpu.VMEM((8, PEERS, 8, 128), F32),
            pltpu.VMEM((ROUNDS, 2, 4, *row), F32),
            pltpu.VMEM((ROUNDS, 2, 4, *row), F32),
            pltpu.VMEM((ROUNDS, 2, *row), F32),
            pltpu.VMEM((ROUNDS, SLABS, *row), F32),
            pltpu.VMEM((4, MODES, NZ), F32),
            pltpu.VMEM((SLABS, 4, MODES, NZ), F32),
            pltpu.VMEM((SLABS, 8, 128), F32),
            pltpu.VMEM((SLABS, 8, 128), F32),
            dma((8,)),
            dma((8,)),
            dma((ROUNDS, 2)),
            dma((ROUNDS, 2)),
            dma((ROUNDS,)),
            dma((ROUNDS,)),
            dma((4,)),
        ],
        compiler_params=pltpu.CompilerParams(
            collective_id=0, has_side_effects=True, vmem_limit_bytes=60 * 1024 * 1024
        ),
        name="channel_adjoint",
    )(
        initial_state,
        drag_rate,
        wall_control,
        lift_profile,
        schur_inverse,
        jnp.asarray(base_table(NX, 1.0 / math.sqrt(NX))),
        jnp.asarray(base_table(NZ, 1.0 / math.sqrt(NZ))),
    )


def solution(mesh):
    return jax.shard_map(
        per_device,
        mesh=mesh,
        in_specs=(
            P(None, None, "gy", "xz", None),
            P("gy", "xz", None),
            P("xz", None),
            P(),
            P("gy", None, "xz", None),
        ),
        out_specs=(P(None, None, "gy", "xz", None), P("xz", "gy")),
        check_vma=False,
    )
```

time: 778 us -> 164 us (0.21); the launches traced: 766 us -> 164 us
  matrix products: 232 us -> 0 us
  Pallas kernels: 0 us -> 160 us
  local copies, waits for them, and re-layouts: 155 us -> 2.69 us
  starting transfers between devices: 132 us -> 0 us
  waiting for transfers between devices: 112 us -> 0 us
  blocking collectives: 91.5 us -> 0 us
  other arithmetic: 39.9 us -> 0 us
    dot_general x32 -> x0, matrix products: 232 us -> none  [the longest x4 39.7 us: to_physical(): jnp.einsum('ykz,nk->yzn', weighted[1], sin_x, precision=HIGHEST)]
    pallas_call x0 -> x1, Pallas kernels: none -> 160 us  [per_device(): pl.pallas_call(kernel, out_shape=(jax.ShapeDtypeStruct((3, 2, ROWS, MODES...]
    all_to_all x12 -> x0, starting transfers between devices: 96.6 us -> none  [the longest x4 43.8 us: to_spectral(): lax.all_to_all(halfway, 'xz', split_axis=3, concat_axis=2, tiled=True)]
    all_to_all x12 -> x0, waiting for transfers between devices: 94.8 us -> none  [the longest x4 51.8 us: copy_for_each(): return lax.all_to_all(copies, axis, split_axis=0, concat_axis=0, tiled=True)]
    all_to_all x5 -> x0, blocking collectives: 91.5 us -> none  [the longest x4 73.4 us: copy_for_each(): return lax.all_to_all(copies, axis, split_axis=0, concat_axis=0, tiled=True)]
    all_to_all x16 -> x0, local copies, waits for them, and re-layouts: 65.4 us -> none  [the longest x9 33.4 us: to_physical(): lax.all_to_all(halfway, 'xz', split_axis=3, concat_axis=2, tiled=True)]
    unnamed x176 -> x4, local copies, waits for them, and re-layouts: 55 us -> 2.69 us
    ppermute x16 -> x0, starting transfers between devices: 35.7 us -> none  [the longest x8 25.4 us: padded(): lax.ppermute(tail, axis, [(i, (i + 1) % count) for i in range(ends)])]
  transfers between devices with their start and end apart: 28 -> 0, of which waited for: 17 -> 0; matrix products, arithmetic and copies ran while one was open for 11% -> 0% of each run, Pallas kernels for 0% -> 0%
where the time goes in v1:
time: 164 us
  Pallas kernels  160 us (98%)
  local copies, waits for them, and re-layouts  2.69 us (2%)
    pallas_call x1, Pallas kernels, per_device(): pl.pallas_call(kernel, out_shape=(jax.ShapeDtypeStruct((3, 2, ROWS, MODES...  160 us

profile of v1, /device:TPU:1, one launch (start us, length us, event | category | flops | bytes accessed | tf_op | source)
XLA Modules:
  0.0 163.7 jit_solution(18190331505381781104)
XLA Ops:
  0.6 160.4 %channel_adjoint.1 = (f32[3,2,8,8,512]{4,3,2,1,0:T(8,128)}, f32[8,128]{1,0:T(8,128)}) custom-call(f32[3,2,8,8,512]{4,3,2,1,0:T(8,128)} %state_in.1, f32[8,8,1024]{2,1,0:T(8,128)} %drag_in.1, f32[8,1024]{1,0:T(8,128)} %ctrl_in.1, f32[64]{0:T(128)} %lift_ref.1, f32[8,8,8,512]{3,2,1,0:T(8,128)} %schur.1, f32[96,512]{1,0:T(8,128)} %constant.4.clone.base_x, ...), custom_call_target="tpu_custom_call" | custom-call | tf_op jit(solution)/shard_map/channel_adjoint/pallas_call | solution.py:474
  161.0 0.0 copy-start
  161.0 2.1 %copy.11 = f32[3,2,8,8,512]{4,3,2,1,0:T(8,128)} copy(f32[3,2,8,8,512]{4,3,2,1,0:T(8,128)} %get-tuple-element.4) | data formatting | bytes 1572864
  163.1 0.0 copy-done
  163.1 0.6 copy.12
Async XLA Ops:
  161.0 2.1 %copy-start = (f32[8,128]{1,0:T(8,128)S(1)}, f32[8,128]{1,0:T(8,128)}, u32[]{:S(2)}) copy-start(f32[8,128]{1,0:T(8,128)} %get-tuple-element.5) | copy-start | bytes 12292

commit v2 on v1

v2 whole, which is shorter than its diff:
```python
import functools
import math

import jax
import jax.numpy as jnp
import numpy as np
from jax import lax
from jax.experimental import pallas as pl
from jax.experimental.pallas import tpu as pltpu
from jax.sharding import PartitionSpec as P

MESH = pl.DeviceIdType.MESH
F32 = jnp.float32
BF16 = jnp.bfloat16
DIFFUSION = 0.04
NX = 1024
NZ = 512
KX = 512
ROWS = 8
MODES = 8
PEERS = 64
SLABS = 8
ROUNDS = 4
CONTROL_SLOT = 6
ORDER = (0, 1)


def base_table(period, scale):
    k = np.arange(512)
    high = 2.0 * np.pi * ((32 * np.arange(16)[:, None] * k) % period) / period
    low = 2.0 * np.pi * ((np.arange(32)[:, None] * k) % period) / period
    return np.concatenate(
        [np.cos(high), np.sin(high), np.cos(low) * scale, np.sin(low) * scale]
    ).astype(np.float32)


def split(x):
    hi = x.astype(BF16)
    return hi, (x - hi.astype(F32))


def regrouped(tiles, lane):
    tiles = [pltpu.roll(tiles[-j % 16], 8 * (-j % 16), 1) if j else tiles[0] for j in range(16)]
    for bit in range(4):
        step = 1 << bit
        chosen = (lane // (8 * step)) % 2 == 1
        tiles = [jnp.where(chosen, tiles[(g - step) % 16], tiles[g]) for g in range(16)]
    return [pltpu.roll(tile, 128 - 8 * g, 1) if g else tile for g, tile in enumerate(tiles)]


def kernel(
    state_hbm, drag_hbm, ctrl_hbm, lift_ref, schur_hbm, base_x_hbm, base_z_hbm,
    out_state, out_grad,
    st, pu, pv, pw, divb, direct, pbuf, wall, chat, zin, zout,
    schur, drag_in, ctrl_in, base_x, base_z, txi, tx, tzh, tzl, dg, waves, amat,
    send, recv, hsend, hrecv, ssend, srecv, gsend, grecv, corner, fsend, frecv, csend, crecv,
    send_sem, recv_sem, hsend_sem, hrecv_sem, ssend_sem, srecv_sem, misc_sem, load_sem,
):
    me = lax.axis_index("xz")
    slab = lax.axis_index("gy")
    barrier = pltpu.get_barrier_semaphore()
    loads = [pltpu.make_async_copy(base_z_hbm, base_z, load_sem.at[0])]
    for comp in range(3):
        for c in range(2):
            loads.append(
                pltpu.make_async_copy(
                    state_hbm.at[comp, c],
                    st.at[comp, pl.ds(2, ROWS), c],
                    load_sem.at[1 + 2 * comp + c],
                )
            )
    for k, (source, target) in enumerate(
        ((base_x_hbm, base_x), (drag_hbm, drag_in), (ctrl_hbm, ctrl_in), (schur_hbm, schur))
    ):
        loads.append(pltpu.make_async_copy(source, target, load_sem.at[7 + k]))
    for load in loads:
        load.start()

    @pl.loop(1, PEERS)
    def _(i):
        pl.semaphore_signal(
            barrier, inc=1, device_id=(lax.rem(me + i, PEERS), slab), device_id_type=MESH
        )

    @pl.loop(1, SLABS)
    def _(i):
        pl.semaphore_signal(
            barrier, inc=1, device_id=(me, lax.rem(slab + i, SLABS)), device_id_type=MESH
        )

    lane = lax.broadcasted_iota(jnp.int32, (8, 128), 1)
    wide_lane = lax.broadcasted_iota(jnp.int32, (KX, 128), 1)
    left = wide_lane < 64
    left_half = left[0:256]
    odd_half = lax.broadcasted_iota(jnp.int32, (256, 128), 0) % 2 == 1
    odd = lax.broadcasted_iota(jnp.int32, (KX, 128), 0) % 2 == 1

    mode = me * MODES + lax.broadcasted_iota(jnp.int32, (MODES, NZ), 0)
    span = lax.broadcasted_iota(jnp.int32, (MODES, NZ), 1)
    kx = (2.0 * math.pi / NX) * mode.astype(F32)
    signed = jnp.where(span < NZ // 2, span, span - NZ)
    kz = jnp.where(span == NZ // 2, 0.0, (2.0 * math.pi / NZ) * signed.astype(F32))
    waves[0] = kx
    waves[1] = kz
    waves[2] = kx * kx + kz * kz
    waves[3] = jnp.where(mode == 0, 1.0, 2.0).astype(F32)

    def turns(base, i):
        ca = base[pl.ds(i, 1), :]
        sa = base[pl.ds(16 + i, 1), :]
        cb = base[32:64, :]
        sb = base[64:96, :]
        c_hi, c_lo = split(ca * cb - sa * sb)
        s_hi, s_lo = split(sa * cb + ca * sb)
        return c_hi, c_lo.astype(BF16), s_hi, s_lo.astype(BF16)

    loads[0].wait()

    @pl.loop(0, 16)
    def _(i):
        rows = pl.ds(pl.multiple_of(i * 32, 32), 32)
        tzh[rows, 0:512], tzl[rows, 0:512], tzh[rows, 512:1024], tzl[rows, 512:1024] = turns(
            base_z, i
        )

    def prepare():
        loads[7].wait()

        @pl.loop(0, 16)
        def _(i):
            c_hi, c_lo, s_hi, s_lo = turns(base_x, i)
            rows = pl.ds(pl.multiple_of(i * 32, 32), 32)
            low_rows = pl.ds(pl.multiple_of(512 + i * 32, 32), 32)
            for h in range(2):
                half = slice(256 * h, 256 * h + 256)
                txi[h, rows, 0:256] = c_hi[:, half]
                txi[h, rows, 256:512] = s_hi[:, half]
                txi[h, low_rows, 0:256] = c_lo[:, half]
                txi[h, low_rows, 256:512] = s_lo[:, half]
            for k, part in enumerate((c_hi, c_lo, s_hi, s_lo)):
                start = pl.multiple_of(256 * k + lax.rem(i, 8) * 32, 32)
                tx[i // 8, pl.ds(start, 32)] = part

        loads[8].wait()
        for b in range(4):
            lo = drag_in[:, :, 128 * b : 128 * b + 128].reshape(64, 128)
            hi = drag_in[:, :, 512 + 128 * b : 640 + 128 * b].reshape(64, 128)
            dg[128 * b : 128 * b + 128, :] = jnp.concatenate([lo, hi], axis=0).T

        loads[9].wait()
        for b in range(4):
            near = ctrl_in[:, 128 * b : 128 * b + 128]
            far = ctrl_in[:, 512 + 128 * b : 640 + 128 * b]
            blank = jnp.zeros((56, 128), F32)
            pieces = jnp.concatenate([near, blank, far, blank], axis=0)
            send[CONTROL_SLOT, 16 * b : 16 * b + 16] = pieces.T.reshape(16, 8, 128)
        x_forward(send[CONTROL_SLOT].reshape(KX, 128), CONTROL_SLOT)
        loads[10].wait()
        gsend[0] = schur[0, 7]
        gsend[1] = schur[7, 0]
        gsend[2] = schur[0, 0]
        gsend[3] = schur[7, 7]
        to_slabs(
            lambda peer: gsend.at[pl.ds(0, 3)],
            grecv.at[slab],
            misc_sem.at[0],
            misc_sem.at[1],
        )
        pltpu.make_async_remote_copy(
            src_ref=gsend.at[3],
            dst_ref=corner,
            send_sem=misc_sem.at[4],
            recv_sem=misc_sem.at[5],
            device_id=(me, lax.rem(slab + 1, SLABS)),
            device_id_type=MESH,
        ).start()

    def x_part(value, h):
        hi = value.astype(BF16).astype(F32)
        lo = value - hi
        real = jnp.where(left_half, hi, pltpu.roll(lo, 64, 1))
        imag = -jnp.where(left_half, pltpu.roll(hi, 64, 1), lo)
        rc = jnp.concatenate([real, jnp.where(odd_half, -real, real)], axis=1)
        rs = jnp.concatenate([imag, jnp.where(odd_half, -imag, imag)], axis=1)
        both = jnp.concatenate([rc, rs], axis=0).astype(BF16)
        out = jnp.dot(txi[h], both, preferred_element_type=F32)
        return out[0:KX] + out[KX : 2 * KX]

    def x_folded(out):
        near, far = out[:, 0:128], out[:, 128:256]
        near = near + pltpu.roll(near, 64, 1)
        far = far + pltpu.roll(far, 64, 1)
        return jnp.where(left, near, far)

    def x_inverse(slot):
        out = None
        for hh in ORDER:
            h = (me // 32) ^ hh
            arrived(slot, h, hh == 0)
            part = x_part(recv[slot, pl.ds(h * 32, 32)].reshape(256, 128), h)
            out = part if out is None else out + part
        return x_folded(out)

    def x_forward(value, slot):
        turned = pltpu.roll(value, 64, 1)
        total = value + turned
        gap = jnp.where(left, value - turned, turned - value)

        def packed(part):
            hi = part.astype(BF16).astype(F32)
            return jnp.where(left, hi, part - hi)

        ra = jnp.concatenate([packed(total), packed(gap)], axis=1).astype(BF16)
        def folded(part):
            part = jnp.where(odd_half, part[:, 128:256], part[:, 0:128])
            return part + pltpu.roll(part, 64, 1)

        for hh in (1, 0):
            h = (me // 32) ^ hh
            out = jnp.dot(tx[h], ra, preferred_element_type=F32)
            with_cos = folded(out[0:256] + out[256:512])
            with_sin = folded(out[512:768] + out[768:1024])
            result = jnp.where(left_half, with_cos, -with_sin)
            send[slot, pl.ds(h * 32, 32)] = result.reshape(32, 8, 128)
            exchange(slot, h, hh == 0)

    def z_dot(value, rows):
        count = value.shape[0]
        hi, lo = split(value)
        both = jnp.concatenate([hi, lo.astype(BF16)], axis=0)
        out = jnp.dot(both, tzh[rows, :], preferred_element_type=F32)
        out = out[0:count] + out[count : 2 * count]
        return out + jnp.dot(hi, tzl[rows, :], preferred_element_type=F32)

    def z_inverse(value, slot):
        out = z_dot(value, slice(0, NZ)).reshape(ROWS, 2, MODES, 2 * NZ)
        with_cos, with_sin = out[:, :, :, 0:NZ], out[:, :, :, NZ : 2 * NZ]
        zout[:, 0] = with_cos[:, 0] - with_sin[:, 1]
        zout[:, 1] = with_sin[:, 0] + with_cos[:, 1]

        for hh in (1, 0):
            h = (me // 32) ^ hh
            for j in range(2):
                block = 2 * h + j
                lanes = pl.ds(pl.multiple_of(block * 128, 128), 128)
                tiles = [zout[a % 8, a // 8, :, lanes] for a in range(16)]
                for g, tile in enumerate(regrouped(tiles, lane)):
                    send[slot, block * 16 + g] = tile
            exchange(slot, h, hh == 0)

    def z_forward(slot):
        out = None
        for hh in ORDER:
            h = (me // 32) ^ hh
            arrived(slot, h, hh == 0)
            half = pl.ds(pl.multiple_of(h * 256, 256), 256)
            for j in range(2):
                block = 2 * h + j
                lanes = pl.ds(pl.multiple_of(block * 128, 128), 128)
                tiles = [recv[slot, block * 16 + g] for g in range(16)]
                for a, tile in enumerate(regrouped(tiles, lane)):
                    zin[a % 8, a // 8, :, lanes] = tile
            part = z_dot(zin[:, :, :, half].reshape(128, 256), half)
            out = part if out is None else out + part
        out = out.reshape(ROWS, 2, MODES, 2 * NZ)
        with_cos, with_sin = out[:, :, :, 0:NZ], out[:, :, :, NZ : 2 * NZ]
        zout[:, 0] = with_cos[:, 0] + with_sin[:, 1]
        zout[:, 1] = with_cos[:, 1] - with_sin[:, 0]

    def exchange(slot, h, own):
        for i in range(31, 0 if own else -1, -1):
            peer = h * 32 + (lax.rem(me, 32) ^ i)
            pltpu.make_async_remote_copy(
                src_ref=send.at[slot, peer],
                dst_ref=recv.at[slot, me],
                send_sem=send_sem.at[slot],
                recv_sem=recv_sem.at[slot, me // 32],
                device_id=(peer, slab),
                device_id_type=MESH,
            ).start()
        if own:
            recv[slot, me] = send[slot, me]

    def arrived(slot, h, own):
        whole = recv.at[slot, pl.ds(0, 31 if own else 32)]
        pltpu.make_async_copy(whole, whole, recv_sem.at[slot, h]).wait()

    def left_device(buffer, sem, count):
        whole = buffer.at[pl.ds(0, count)]
        pltpu.make_async_copy(whole, whole, sem).wait()

    def to_slabs(source, target, out_sem, in_sem):
        @pl.loop(1, SLABS)
        def _(i):
            peer = lax.rem(slab + i, SLABS)
            pltpu.make_async_remote_copy(
                src_ref=source(peer),
                dst_ref=target,
                send_sem=out_sem,
                recv_sem=in_sem,
                device_id=(me, peer),
                device_id_type=MESH,
            ).start()

    pl.semaphore_wait(barrier, PEERS - 1 + SLABS - 1)

    loads[1].wait()
    loads[2].wait()
    wall[...] = jnp.zeros_like(wall)

    @pl.loop(0, ROUNDS)
    def _(r):
        adjoint = r // 2
        moving = r != 2
        rate = jnp.where(moving, DIFFUSION, 0.0).astype(F32)

        @pl.when(r == 0)
        def _():
            for load in loads[3:7]:
                load.wait()

        for side, (u_row, v_row) in enumerate(((9, 8), (2, 2))):
            hsend[r, side, 0] = st[0, u_row]
            hsend[r, side, 1] = st[1, v_row]
            hsend[r, side, 2] = st[1, v_row + 1]
            hsend[r, side, 3] = st[2, u_row]
        def send_halo(part):
            for side in range(2):
                rows = part(side)
                pltpu.make_async_remote_copy(
                    src_ref=hsend.at[r, side, rows],
                    dst_ref=hrecv.at[r, side, rows],
                    send_sem=hsend_sem.at[r, side],
                    recv_sem=hrecv_sem.at[r, side],
                    device_id=(me, lax.rem(slab + (1 if side == 0 else SLABS - 1), SLABS)),
                    device_id_type=MESH,
                ).start()

        def wait_halo(part, buffer, sem):
            for side in range(2):
                whole = buffer.at[r, side, part(side)]
                pltpu.make_async_copy(whole, whole, sem.at[r, side]).wait()

        def all_rows(side):
            return pl.ds(0, 4)

        def near_row(side):
            return pl.ds(2 - side, 1)

        @pl.when(moving)
        def _():
            send_halo(all_rows)

        @pl.when(r == 2)
        def _():
            send_halo(near_row)

        @pl.when(moving)
        def _():
            before = jnp.where(r < 2, waves[3], 1.0)
            z_inverse((st[0, 2:10] * before).reshape(128, NZ), 2 * jnp.where(r == 3, 2, r))

        @pl.when(r == 0)
        def _():
            prepare()

        @pl.when(moving)
        def _():
            wait_halo(all_rows, hrecv, hrecv_sem)
            for side, (u_row, v_row, edge) in enumerate(((1, 0, 0), (10, 10, SLABS - 1))):
                open_side = slab != edge
                st[0, u_row] = jnp.where(open_side, hrecv[r, side, 0], 0.0)
                st[1, v_row] = jnp.where(open_side, hrecv[r, side, 1], 0.0)
                st[1, v_row + 1] = jnp.where(open_side, hrecv[r, side, 2], 0.0)
                st[2, u_row] = jnp.where(open_side, hrecv[r, side, 3], 0.0)

        @pl.when(r == 2)
        def _():
            wait_halo(near_row, hrecv, hrecv_sem)
            for side, (v_row, edge) in enumerate(((1, 0), (10, SLABS - 1))):
                st[1, v_row] = jnp.where(slab != edge, hrecv[r, side, 2 - side], 0.0)

        square = waves[2]

        def diffused(comp, row):
            middle = st[comp, row]
            around = st[comp, row + 1] - 2.0 * middle + st[comp, row - 1]
            return middle + rate * (around - square * middle)

        @pl.loop(0, ROWS)
        def _(y):
            pu[y] = diffused(0, y + 2)
            pw[y] = diffused(2, y + 2)

        @pl.loop(0, ROWS + 2)
        def _(y):
            row = slab * ROWS + y - 1
            inside = jnp.logical_and(row >= 0, row < ROWS * SLABS)
            pv[y] = jnp.where(inside, diffused(1, y + 1), 0.0)

        @pl.when(moving)
        def _():
            slot = 2 * jnp.where(r == 3, 2, r)
            x_forward(x_inverse(slot) * dg[...], slot + 1)

        @pl.when(r == 0)
        def _():
            z_forward(CONTROL_SLOT)
            chat[...] = zout[0]
            pltpu.make_async_copy(
                grecv.at[pl.ds(0, SLABS - 1)], grecv.at[pl.ds(0, SLABS - 1)], misc_sem.at[1]
            ).wait()
            pltpu.make_async_copy(corner, corner, misc_sem.at[5]).wait()

            def gather_a(i, a):
                b = SLABS - 1 - i
                return grecv[b, 2] + grecv[b, 0] * a * grecv[b, 1]

            amat[...] = lax.fori_loop(0, SLABS - 1 - slab, gather_a, jnp.zeros((MODES, NZ), F32))

        @pl.when(r < 2)
        def _():
            @pl.loop(0, ROWS + 2)
            def _(y):
                row = slab * ROWS + y - 1
                inside = jnp.logical_and(row >= 0, row < ROWS * SLABS)
                safe = jnp.clip(row, 0, ROWS * SLABS - 1)
                level = jnp.where(inside, lift_ref[safe], 0.0)
                pv[y] = pv[y] + level * chat[...]

        kxv, kzv = waves[0], waves[1]

        @pl.when(moving)
        def _():
            slot = 2 * jnp.where(r == 3, 2, r) + 1
            z_forward(slot)
            after = jnp.where(r < 2, 1.0, waves[3])

            @pl.loop(0, ROWS)
            def _(y):
                pu[y] = pu[y] - zout[y] * after

        @pl.loop(0, ROWS)
        def _(y):
            slope = 0.5 * (pv[y + 2] - pv[y])
            divb[y, 0] = slope[0] - kxv * pu[y, 1] - kzv * pw[y, 1]
            divb[y, 1] = slope[1] + kxv * pu[y, 0] + kzv * pw[y, 0]

        def entry(i, j):
            return schur[i + adjoint * (j - i), j + adjoint * (i - j)]

        def solve_row(i):
            total = entry(i, 0) * divb[0]
            for j in range(1, ROWS):
                total = total + entry(i, j) * divb[j]
            direct[i] = total

        @pl.loop(0, 2)
        def _(i):
            solve_row(7 * i)

        ratio = entry(7, 0)
        turn = entry(0, 7)
        last = direct[7]
        ssend[r, 0] = last
        ssend[r, 1] = direct[0] + turn * (amat[...] * last)
        to_slabs(
            lambda peer: ssend.at[r, jnp.where(peer > slab, 0, 1)],
            srecv.at[r, slab],
            ssend_sem.at[r],
            srecv_sem.at[r],
        )

        @pl.loop(1, ROWS - 1)
        def _(i):
            solve_row(i)

        whole = srecv.at[r, pl.ds(0, SLABS - 1)]
        pltpu.make_async_copy(whole, whole, srecv_sem.at[r]).wait()

        blank = jnp.zeros((2, MODES, NZ), F32)
        entering = lax.fori_loop(
            0, slab, lambda b, z: srecv[r, b] + grecv[b, 1 - adjoint] * z, blank
        )

        def suffix(i, e):
            b = SLABS - 1 - i
            return srecv[r, b] + grecv[b, adjoint] * e

        above = lax.fori_loop(0, SLABS - 1 - slab, suffix, blank)
        leaving = above + amat[...] * (last + ratio * entering)
        pbuf[9] = leaving

        @pl.loop(0, ROWS)
        def _(i):
            pbuf[i + 1] = direct[i] + entry(i, 0) * entering + entry(i, 7) * leaving

        pbuf[0] = jnp.where(slab == 0, 0.0, entering + corner[...] * pbuf[1])

        @pl.loop(0, ROWS)
        def _(y):
            p0, p1 = pbuf[y + 1, 0], pbuf[y + 1, 1]
            st[0, y + 2, 0] = pu[y, 0] + kxv * p1
            st[0, y + 2, 1] = pu[y, 1] - kxv * p0
            st[2, y + 2, 0] = pw[y, 0] + kzv * p1
            st[2, y + 2, 1] = pw[y, 1] - kzv * p0
            normal = pv[y + 1] - 0.5 * (pbuf[y + 2] - pbuf[y])
            st[1, y + 2] = normal
            level = jnp.where(r >= 2, lift_ref[slab * ROWS + y], 0.0)
            wall[...] = wall[...] + level * normal

        @pl.when(r == 1)
        def _():
            @pl.loop(0, ROWS)
            def _(y):
                for comp in range(3):
                    for c in range(2):
                        out_state[comp, c, y] = st[comp, y + 2, c]

    out = z_dot(wall[...].reshape(16, NZ), slice(0, NZ))
    rows16 = jnp.concatenate(
        [out[0:8, 0:NZ] - out[8:16, NZ:], out[0:8, NZ:] + out[8:16, 0:NZ]], axis=0
    )
    row16 = lax.broadcasted_iota(jnp.int32, (16, 128), 0)
    lane16 = lax.broadcasted_iota(jnp.int32, (16, 128), 1) // 8
    for block in range(4):
        piece = rows16[:, 128 * block : 128 * block + 128]
        for bit in range(4):
            step = 1 << bit
            piece = jnp.where(
                (row16 // step) % 2 == 1, pltpu.roll(piece, 128 - 8 * step, 1), piece
            )
        for bit in range(4):
            step = 1 << bit
            piece = jnp.where((lane16 // step) % 2 == 1, pltpu.roll(piece, step, 0), piece)
        for g in range(16):
            csend[16 * block + g] = piece[g : g + 1]

    for i in range(PEERS - 1, 0, -1):
        peer = me ^ i
        pltpu.make_async_remote_copy(
            src_ref=csend.at[peer],
            dst_ref=crecv.at[me],
            send_sem=misc_sem.at[6],
            recv_sem=misc_sem.at[7],
            device_id=(peer, slab),
            device_id_type=MESH,
        ).start()
    crecv[me] = csend[me]
    left_device(crecv, misc_sem.at[7], PEERS - 1)
    plane = jnp.broadcast_to(crecv[...], (PEERS, 8, 128)).reshape(KX, 128)
    plane = pltpu.roll(plane, lax.rem(128 - 8 * lax.rem(me, 16), 128), 1)
    rank = lax.broadcasted_iota(jnp.int32, (KX, 128), 0)
    for bit in range(3):
        step = 1 << bit
        plane = jnp.where((rank // step) % 2 == 1, pltpu.roll(plane, 8 * step, 1), plane)
    plane = x_folded(x_part(plane[0:256], 0) + x_part(plane[256:512], 1))
    for b in range(4):
        turned = plane[128 * b : 128 * b + 128, :].T
        fsend[b] = turned[0:8]
        fsend[4 + b] = turned[64:72]
    to_slabs(
        lambda peer: fsend.at[peer], frecv.at[slab], misc_sem.at[2], misc_sem.at[3]
    )
    frecv[slab] = fsend[slab]
    left_device(frecv, misc_sem.at[3], SLABS - 1)
    total = frecv[0]
    for b in range(1, SLABS):
        total = total + frecv[b]
    out_grad[...] = total

    @pl.loop(0, 7)
    def _(slot):
        left_device(send.at[slot], send_sem.at[slot], PEERS - 1)

    @pl.loop(0, ROUNDS)
    def _(r):
        left_device(srecv.at[r], ssend_sem.at[r], SLABS - 1)
        for side in range(2):
            @pl.when(r != 2)
            def _():
                whole = hsend.at[r, side]
                pltpu.make_async_copy(whole, whole, hsend_sem.at[r, side]).wait()

            @pl.when(r == 2)
            def _():
                whole = hsend.at[r, side, pl.ds(0, 1)]
                pltpu.make_async_copy(whole, whole, hsend_sem.at[r, side]).wait()

    left_device(grecv, misc_sem.at[0], SLABS - 1)
    pltpu.make_async_copy(corner, corner, misc_sem.at[4]).wait()
    left_device(frecv, misc_sem.at[2], SLABS - 1)
    left_device(crecv, misc_sem.at[6], PEERS - 1)


def per_device(initial_state, drag_rate, wall_control, lift_profile, schur_inverse):
    row = (2, MODES, NZ)
    vmem = pl.BlockSpec(memory_space=pltpu.VMEM)
    hbm = pl.BlockSpec(memory_space=pl.ANY)
    smem = pl.BlockSpec(memory_space=pltpu.SMEM)
    dma = pltpu.SemaphoreType.DMA
    return pl.pallas_call(
        kernel,
        out_shape=(
            jax.ShapeDtypeStruct((3, 2, ROWS, MODES, NZ), F32),
            jax.ShapeDtypeStruct((8, 128), F32),
        ),
        in_specs=[hbm, hbm, hbm, smem, hbm, hbm, hbm],
        out_specs=(vmem, vmem),
        scratch_shapes=[
            pltpu.VMEM((3, ROWS + 4, *row), F32),
            pltpu.VMEM((ROWS, *row), F32),
            pltpu.VMEM((ROWS + 2, *row), F32),
            pltpu.VMEM((ROWS, *row), F32),
            pltpu.VMEM((ROWS, *row), F32),
            pltpu.VMEM((ROWS, *row), F32),
            pltpu.VMEM((ROWS + 2, *row), F32),
            pltpu.VMEM(row, F32),
            pltpu.VMEM(row, F32),
            pltpu.VMEM((ROWS, *row), F32),
            pltpu.VMEM((ROWS, *row), F32),
            pltpu.VMEM((ROWS, ROWS, MODES, NZ), F32),
            pltpu.VMEM((ROWS, MODES, NX), F32),
            pltpu.VMEM((8, NX), F32),
            pltpu.VMEM((96, 512), F32),
            pltpu.VMEM((96, 512), F32),
            pltpu.VMEM((2, 1024, 512), BF16),
            pltpu.VMEM((2, 1024, 512), BF16),
            pltpu.VMEM((512, 1024), BF16),
            pltpu.VMEM((512, 1024), BF16),
            pltpu.VMEM((512, 128), F32),
            pltpu.VMEM((4, MODES, NZ), F32),
            pltpu.VMEM((MODES, NZ), F32),
            pltpu.VMEM((7, PEERS, 8, 128), F32),
            pltpu.VMEM((7, PEERS, 8, 128), F32),
            pltpu.VMEM((ROUNDS, 2, 4, *row), F32),
            pltpu.VMEM((ROUNDS, 2, 4, *row), F32),
            pltpu.VMEM((ROUNDS, 2, *row), F32),
            pltpu.VMEM((ROUNDS, SLABS, *row), F32),
            pltpu.VMEM((4, MODES, NZ), F32),
            pltpu.VMEM((SLABS, 3, MODES, NZ), F32),
            pltpu.VMEM((MODES, NZ), F32),
            pltpu.VMEM((SLABS, 8, 128), F32),
            pltpu.VMEM((SLABS, 8, 128), F32),
            pltpu.VMEM((PEERS, 1, 128), F32),
            pltpu.VMEM((PEERS, 1, 128), F32),
            dma((7,)),
            dma((7, 2)),
            dma((ROUNDS, 2)),
            dma((ROUNDS, 2)),
            dma((ROUNDS,)),
            dma((ROUNDS,)),
            dma((8,)),
            dma((11,)),
        ],
        compiler_params=pltpu.CompilerParams(
            collective_id=0, has_side_effects=True, vmem_limit_bytes=60 * 1024 * 1024
        ),
        name="channel_adjoint",
    )(
        initial_state,
        drag_rate,
        wall_control,
        lift_profile,
        schur_inverse,
        jnp.asarray(base_table(NX, 1.0 / math.sqrt(NX))),
        jnp.asarray(base_table(NZ, 1.0 / math.sqrt(NZ))),
    )


def solution(mesh):
    return jax.shard_map(
        per_device,
        mesh=mesh,
        in_specs=(
            P(None, None, "gy", "xz", None),
            P("gy", "xz", None),
            P("xz", None),
            P(),
            P("gy", None, "xz", None),
        ),
        out_specs=(P(None, None, "gy", "xz", None), P("xz", "gy")),
        check_vma=False,
    )
```

time: 164 us -> 139 us (0.85)
  Pallas kernels: 160 us -> 136 us
    pallas_call x1, Pallas kernels: 160 us -> 136 us  [per_device(): pl.pallas_call(kernel, out_shape=(jax.ShapeDtypeStruct((3, 2, ROWS, MODES...]
where the time goes in v2:
time: 139 us
  Pallas kernels  136 us (98%)
  local copies, waits for them, and re-layouts  2.69 us (2%)
    pallas_call x1, Pallas kernels, per_device(): pl.pallas_call(kernel, out_shape=(jax.ShapeDtypeStruct((3, 2, ROWS, MODES...  136 us

profile of v2, /device:TPU:1, one launch (start us, length us, event | category | flops | bytes accessed | tf_op | source)
XLA Modules:
  0.0 139.1 jit_solution(6404460791152599618)
XLA Ops:
  0.6 135.8 %channel_adjoint.1 = (f32[3,2,8,8,512]{4,3,2,1,0:T(8,128)}, f32[8,128]{1,0:T(8,128)}) custom-call(f32[3,2,8,8,512]{4,3,2,1,0:T(8,128)} %state_hbm.1, f32[8,8,1024]{2,1,0:T(8,128)} %drag_hbm.1, f32[8,1024]{1,0:T(8,128)} %ctrl_hbm.1, f32[64]{0:T(128)} %lift_ref.1, f32[8,8,8,512]{3,2,1,0:T(8,128)} %schur_hbm.1, f32[96,512]{1,0:T(8,128)} %constant.4.clone.base_x_hbm, ...), custom_call_target="tpu_custom_call" | custom-call | tf_op jit(solution)/shard_map/channel_adjoint/pallas_call | solution.py:602
  136.4 0.0 copy-start
  136.4 2.1 %copy.11 = f32[3,2,8,8,512]{4,3,2,1,0:T(8,128)} copy(f32[3,2,8,8,512]{4,3,2,1,0:T(8,128)} %get-tuple-element.4) | data formatting | bytes 1572864
  138.5 0.0 copy-done
  138.5 0.6 copy.12
Async XLA Ops:
  136.4 2.1 %copy-start = (f32[8,128]{1,0:T(8,128)S(1)}, f32[8,128]{1,0:T(8,128)}, u32[]{:S(2)}) copy-start(f32[8,128]{1,0:T(8,128)} %get-tuple-element.5) | copy-start | bytes 12292

commit v3 on v2

--- a/solution.py
+++ b/solution.py
@@ -75,6 +75,15 @@
         loads.append(pltpu.make_async_copy(source, target, load_sem.at[7 + k]))
     for load in loads:
         load.start()
+    stores = [
+        pltpu.make_async_copy(
+            st.at[comp, pl.ds(2, ROWS), c],
+            out_state.at[comp, c],
+            load_sem.at[11 + 2 * comp + c],
+        )
+        for comp in range(3)
+        for c in range(2)
+    ]
 
     @pl.loop(1, PEERS)
     def _(i):
@@ -131,12 +140,10 @@
             c_hi, c_lo, s_hi, s_lo = turns(base_x, i)
             rows = pl.ds(pl.multiple_of(i * 32, 32), 32)
             low_rows = pl.ds(pl.multiple_of(512 + i * 32, 32), 32)
-            for h in range(2):
-                half = slice(256 * h, 256 * h + 256)
-                txi[h, rows, 0:256] = c_hi[:, half]
-                txi[h, rows, 256:512] = s_hi[:, half]
-                txi[h, low_rows, 0:256] = c_lo[:, half]
-                txi[h, low_rows, 256:512] = s_lo[:, half]
+            txi[rows, 0:512] = c_hi
+            txi[rows, 512:1024] = s_hi
+            txi[low_rows, 0:512] = c_lo
+            txi[low_rows, 512:1024] = s_lo
             for k, part in enumerate((c_hi, c_lo, s_hi, s_lo)):
                 start = pl.multiple_of(256 * k + lax.rem(i, 8) * 32, 32)
                 tx[i // 8, pl.ds(start, 32)] = part
@@ -175,31 +182,25 @@
             device_id_type=MESH,
         ).start()
 
-    def x_part(value, h):
+    def x_part(value):
         hi = value.astype(BF16).astype(F32)
         lo = value - hi
-        real = jnp.where(left_half, hi, pltpu.roll(lo, 64, 1))
-        imag = -jnp.where(left_half, pltpu.roll(hi, 64, 1), lo)
-        rc = jnp.concatenate([real, jnp.where(odd_half, -real, real)], axis=1)
-        rs = jnp.concatenate([imag, jnp.where(odd_half, -imag, imag)], axis=1)
+        real = jnp.where(left, hi, pltpu.roll(lo, 64, 1))
+        imag = -jnp.where(left, pltpu.roll(hi, 64, 1), lo)
+        rc = jnp.concatenate([real, jnp.where(odd, -real, real)], axis=1)
+        rs = jnp.concatenate([imag, jnp.where(odd, -imag, imag)], axis=1)
         both = jnp.concatenate([rc, rs], axis=0).astype(BF16)
-        out = jnp.dot(txi[h], both, preferred_element_type=F32)
-        return out[0:KX] + out[KX : 2 * KX]
-
-    def x_folded(out):
+        out = jnp.dot(txi[...], both, preferred_element_type=F32)
+        out = out[0:KX] + out[KX : 2 * KX]
         near, far = out[:, 0:128], out[:, 128:256]
         near = near + pltpu.roll(near, 64, 1)
         far = far + pltpu.roll(far, 64, 1)
         return jnp.where(left, near, far)
 
     def x_inverse(slot):
-        out = None
         for hh in ORDER:
-            h = (me // 32) ^ hh
-            arrived(slot, h, hh == 0)
-            part = x_part(recv[slot, pl.ds(h * 32, 32)].reshape(256, 128), h)
-            out = part if out is None else out + part
-        return x_folded(out)
+            arrived(slot, (me // 32) ^ hh, hh == 0)
+        return x_part(recv[slot].reshape(KX, 128))
 
     def x_forward(value, slot):
         turned = pltpu.roll(value, 64, 1)
@@ -232,7 +233,7 @@
         out = out[0:count] + out[count : 2 * count]
         return out + jnp.dot(hi, tzl[rows, :], preferred_element_type=F32)
 
-    def z_inverse(value, slot):
+    def z_inverse(value, slot, sent):
         out = z_dot(value, slice(0, NZ)).reshape(ROWS, 2, MODES, 2 * NZ)
         with_cos, with_sin = out[:, :, :, 0:NZ], out[:, :, :, NZ : 2 * NZ]
         zout[:, 0] = with_cos[:, 0] - with_sin[:, 1]
@@ -246,7 +247,8 @@
                 tiles = [zout[a % 8, a // 8, :, lanes] for a in range(16)]
                 for g, tile in enumerate(regrouped(tiles, lane)):
                     send[slot, block * 16 + g] = tile
-            exchange(slot, h, hh == 0)
+            if sent:
+                exchange(slot, h, hh == 0)
 
     def z_forward(slot):
         out = None
@@ -268,7 +270,8 @@
         zout[:, 1] = with_cos[:, 1] - with_sin[:, 0]
 
     def exchange(slot, h, own):
-        for i in range(31, 0 if own else -1, -1):
+        order = [8 * y + x for x in range(8) for y in range(4)][::-1]
+        for i in [k for k in order if k or not own]:
             peer = h * 32 + (lax.rem(me, 32) ^ i)
             pltpu.make_async_remote_copy(
                 src_ref=send.at[slot, peer],
@@ -290,8 +293,7 @@
         pltpu.make_async_copy(whole, whole, sem).wait()
 
     def to_slabs(source, target, out_sem, in_sem):
-        @pl.loop(1, SLABS)
-        def _(i):
+        for i in (4, 3, 5, 2, 6, 1, 7):
             peer = lax.rem(slab + i, SLABS)
             pltpu.make_async_remote_copy(
                 src_ref=source(peer),
@@ -302,10 +304,12 @@
                 device_id_type=MESH,
             ).start()
 
-    pl.semaphore_wait(barrier, PEERS - 1 + SLABS - 1)
-
     loads[1].wait()
     loads[2].wait()
+    z_inverse((st[0, 2:10] * waves[3]).reshape(128, NZ), 0, False)
+    pl.semaphore_wait(barrier, PEERS - 1 + SLABS - 1)
+    for hh in (1, 0):
+        exchange(0, (me // 32) ^ hh, hh == 0)
     wall[...] = jnp.zeros_like(wall)
 
     @pl.loop(0, ROUNDS)
@@ -355,10 +359,11 @@
         def _():
             send_halo(near_row)
 
-        @pl.when(moving)
+        @pl.when(jnp.logical_or(r == 1, r == 3))
         def _():
             before = jnp.where(r < 2, waves[3], 1.0)
-            z_inverse((st[0, 2:10] * before).reshape(128, NZ), 2 * jnp.where(r == 3, 2, r))
+            value = (st[0, 2:10] * before).reshape(128, NZ)
+            z_inverse(value, 2 * jnp.where(r == 3, 2, r), True)
 
         @pl.when(r == 0)
         def _():
@@ -376,9 +381,8 @@
 
         @pl.when(r == 2)
         def _():
-            wait_halo(near_row, hrecv, hrecv_sem)
-            for side, (v_row, edge) in enumerate(((1, 0), (10, SLABS - 1))):
-                st[1, v_row] = jnp.where(slab != edge, hrecv[r, side, 2 - side], 0.0)
+            st[1, 1] = jnp.zeros((2, MODES, NZ), F32)
+            st[1, 10] = jnp.zeros((2, MODES, NZ), F32)
 
         square = waves[2]
 
@@ -461,9 +465,17 @@
 
         ratio = entry(7, 0)
         turn = entry(0, 7)
-        last = direct[7]
-        ssend[r, 0] = last
-        ssend[r, 1] = direct[0] + turn * (amat[...] * last)
+        half = jnp.where(r == 2, 0.5, 0.0).astype(F32)
+        last = direct[7] - half * st[1, 9]
+        first_v = half * st[1, 2]
+        cross = jnp.where(slab == 0, 0.0, corner[...] * first_v)
+        ssend[r, 0] = last + ratio * cross
+        ssend[r, 1] = (
+            direct[0]
+            + turn * (amat[...] * last)
+            + first_v
+            + (schur[0, 0] + turn * amat[...] * ratio) * cross
+        )
         to_slabs(
             lambda peer: ssend.at[r, jnp.where(peer > slab, 0, 1)],
             srecv.at[r, slab],
@@ -482,6 +494,7 @@
         entering = lax.fori_loop(
             0, slab, lambda b, z: srecv[r, b] + grecv[b, 1 - adjoint] * z, blank
         )
+        entering = entering + cross
 
         def suffix(i, e):
             b = SLABS - 1 - i
@@ -496,6 +509,14 @@
             pbuf[i + 1] = direct[i] + entry(i, 0) * entering + entry(i, 7) * leaving
 
         pbuf[0] = jnp.where(slab == 0, 0.0, entering + corner[...] * pbuf[1])
+
+        @pl.when(r == 2)
+        def _():
+            wait_halo(near_row, hrecv, hrecv_sem)
+            pbuf[0] = pbuf[0] + jnp.where(slab == 0, 0.0, 0.5 * hrecv[r, 0, 2])
+            pbuf[9] = pbuf[9] - jnp.where(slab == SLABS - 1, 0.0, 0.5 * hrecv[r, 1, 1])
+            for copy in stores:
+                copy.wait()
 
         @pl.loop(0, ROWS)
         def _(y):
@@ -511,11 +532,8 @@
 
         @pl.when(r == 1)
         def _():
-            @pl.loop(0, ROWS)
-            def _(y):
-                for comp in range(3):
-                    for c in range(2):
-                        out_state[comp, c, y] = st[comp, y + 2, c]
+            for copy in stores:
+                copy.start()
 
     out = z_dot(wall[...].reshape(16, NZ), slice(0, NZ))
     rows16 = jnp.concatenate(
@@ -554,7 +572,7 @@
     for bit in range(3):
         step = 1 << bit
         plane = jnp.where((rank // step) % 2 == 1, pltpu.roll(plane, 8 * step, 1), plane)
-    plane = x_folded(x_part(plane[0:256], 0) + x_part(plane[256:512], 1))
+    plane = x_part(plane)
     for b in range(4):
         turned = plane[128 * b : 128 * b + 128, :].T
         fsend[b] = turned[0:8]
@@ -606,7 +624,7 @@
             jax.ShapeDtypeStruct((8, 128), F32),
         ),
         in_specs=[hbm, hbm, hbm, smem, hbm, hbm, hbm],
-        out_specs=(vmem, vmem),
+        out_specs=(hbm, vmem),
         scratch_shapes=[
             pltpu.VMEM((3, ROWS + 4, *row), F32),
             pltpu.VMEM((ROWS, *row), F32),
@@ -624,7 +642,7 @@
             pltpu.VMEM((8, NX), F32),
             pltpu.VMEM((96, 512), F32),
             pltpu.VMEM((96, 512), F32),
-            pltpu.VMEM((2, 1024, 512), BF16),
+            pltpu.VMEM((1024, 1024), BF16),
             pltpu.VMEM((2, 1024, 512), BF16),
             pltpu.VMEM((512, 1024), BF16),
             pltpu.VMEM((512, 1024), BF16),
@@ -651,7 +669,7 @@
             dma((ROUNDS,)),
             dma((ROUNDS,)),
             dma((8,)),
-            dma((11,)),
+            dma((17,)),
         ],
         compiler_params=pltpu.CompilerParams(
             collective_id=0, has_side_effects=True, vmem_limit_bytes=60 * 1024 * 1024

time: 139 us -> 130 us (0.935)
  Pallas kernels: 136 us -> 127 us
    pallas_call x1, Pallas kernels: 136 us -> 127 us  [per_device(): pl.pallas_call(kernel, out_shape=(jax.ShapeDtypeStruct((3, 2, ROWS, MODES...]
where the time goes in v3:
time: 130 us
  Pallas kernels  127 us (98%)
  local copies, waits for them, and re-layouts  2.69 us (2%)
    pallas_call x1, Pallas kernels, per_device(): pl.pallas_call(kernel, out_shape=(jax.ShapeDtypeStruct((3, 2, ROWS, MODES...  127 us
    unnamed x4, local copies, waits for them, and re-layouts  2.69 us

profile of v3, /device:TPU:1, one launch (start us, length us, event | category | flops | bytes accessed | tf_op | source)
XLA Modules:
  0.0 130.2 jit_solution(16901134621383775492)
XLA Ops:
  0.6 126.9 %channel_adjoint.1 = (f32[3,2,8,8,512]{4,3,2,1,0:T(8,128)}, f32[8,128]{1,0:T(8,128)}) custom-call(f32[3,2,8,8,512]{4,3,2,1,0:T(8,128)} %state_hbm.1, f32[8,8,1024]{2,1,0:T(8,128)} %drag_hbm.1, f32[8,1024]{1,0:T(8,128)} %ctrl_hbm.1, f32[64]{0:T(128)} %lift_ref.1, f32[8,8,8,512]{3,2,1,0:T(8,128)} %schur_hbm.1, f32[96,512]{1,0:T(8,128)} %constant.4.clone.base_x_hbm, ...), custom_call_target="tpu_custom_call" | custom-call | tf_op jit(solution)/shard_map/channel_adjoint/pallas_call | solution.py:620
  127.5 0.0 copy-start
  127.5 2.1 %copy.11 = f32[3,2,8,8,512]{4,3,2,1,0:T(8,128)} copy(f32[3,2,8,8,512]{4,3,2,1,0:T(8,128)} %get-tuple-element.4) | data formatting | bytes 1572864
  129.6 0.0 copy-done
  129.6 0.6 copy.12
Async XLA Ops:
  127.5 2.1 %copy-start = (f32[8,128]{1,0:T(8,128)S(1)}, f32[8,128]{1,0:T(8,128)}, u32[]{:S(2)}) copy-start(f32[8,128]{1,0:T(8,128)} %get-tuple-element.5) | copy-start | bytes 12292

commit v4 on v3

--- a/solution.py
+++ b/solution.py
@@ -59,6 +59,12 @@
     me = lax.axis_index("xz")
     slab = lax.axis_index("gy")
     barrier = pltpu.get_barrier_semaphore()
+    for i in range(PEERS - 1, 0, -1):
+        pl.semaphore_signal(barrier, inc=1, device_id=(me ^ i, slab), device_id_type=MESH)
+    for i in (4, 3, 5, 2, 6, 1, 7):
+        pl.semaphore_signal(
+            barrier, inc=1, device_id=(me, lax.rem(slab + i, SLABS)), device_id_type=MESH
+        )
     loads = [pltpu.make_async_copy(base_z_hbm, base_z, load_sem.at[0])]
     for comp in range(3):
         for c in range(2):
@@ -84,18 +90,6 @@
         for comp in range(3)
         for c in range(2)
     ]
-
-    @pl.loop(1, PEERS)
-    def _(i):
-        pl.semaphore_signal(
-            barrier, inc=1, device_id=(lax.rem(me + i, PEERS), slab), device_id_type=MESH
-        )
-
-    @pl.loop(1, SLABS)
-    def _(i):
-        pl.semaphore_signal(
-            barrier, inc=1, device_id=(me, lax.rem(slab + i, SLABS)), device_id_type=MESH
-        )
 
     lane = lax.broadcasted_iota(jnp.int32, (8, 128), 1)
     wide_lane = lax.broadcasted_iota(jnp.int32, (KX, 128), 1)
@@ -270,7 +264,7 @@
         zout[:, 1] = with_cos[:, 1] - with_sin[:, 0]
 
     def exchange(slot, h, own):
-        order = [8 * y + x for x in range(8) for y in range(4)][::-1]
+        order = [8 * y + x for x in (7, 6, 5, 4, 3, 2, 1, 0) for y in ((3, 2, 1, 0) if own else range(4))]
         for i in [k for k in order if k or not own]:
             peer = h * 32 + (lax.rem(me, 32) ^ i)
             pltpu.make_async_remote_copy(
@@ -554,7 +548,7 @@
         for g in range(16):
             csend[16 * block + g] = piece[g : g + 1]
 
-    for i in range(PEERS - 1, 0, -1):
+    for i in [8 * y + x for x in range(8) for y in range(8)][:0:-1]:
         peer = me ^ i
         pltpu.make_async_remote_copy(
             src_ref=csend.at[peer],

time: 130 us -> 129 us (level)
  no operation moved by 1% of the time
where the time goes in v4:
time: 129 us
  Pallas kernels  126 us (98%)
  local copies, waits for them, and re-layouts  2.69 us (2%)
    pallas_call x1, Pallas kernels, per_device(): pl.pallas_call(kernel, out_shape=(jax.ShapeDtypeStruct((3, 2, ROWS, MODES...  126 us
    unnamed x4, local copies, waits for them, and re-layouts  2.69 us

profile of v4, /device:TPU:1, one launch (start us, length us, event | category | flops | bytes accessed | tf_op | source)
XLA Modules:
  0.0 129.1 jit_solution(6333991592351189061)
XLA Ops:
  0.6 125.8 %channel_adjoint.1 = (f32[3,2,8,8,512]{4,3,2,1,0:T(8,128)}, f32[8,128]{1,0:T(8,128)}) custom-call(f32[3,2,8,8,512]{4,3,2,1,0:T(8,128)} %state_hbm.1, f32[8,8,1024]{2,1,0:T(8,128)} %drag_hbm.1, f32[8,1024]{1,0:T(8,128)} %ctrl_hbm.1, f32[64]{0:T(128)} %lift_ref.1, f32[8,8,8,512]{3,2,1,0:T(8,128)} %schur_hbm.1, f32[96,512]{1,0:T(8,128)} %constant.4.clone.base_x_hbm, ...), custom_call_target="tpu_custom_call" | custom-call | tf_op jit(solution)/shard_map/channel_adjoint/pallas_call | solution.py:614
  126.4 0.0 copy-start
  126.5 2.1 %copy.11 = f32[3,2,8,8,512]{4,3,2,1,0:T(8,128)} copy(f32[3,2,8,8,512]{4,3,2,1,0:T(8,128)} %get-tuple-element.4) | data formatting | bytes 1572864
  128.6 0.0 copy-done
  128.6 0.6 copy.12
Async XLA Ops:
  126.4 2.1 %copy-start = (f32[8,128]{1,0:T(8,128)S(1)}, f32[8,128]{1,0:T(8,128)}, u32[]{:S(2)}) copy-start(f32[8,128]{1,0:T(8,128)} %get-tuple-element.5) | copy-start | bytes 12292
